TPU v7x, 128 devices: a whole 4x4x4 slice. The times are simulated.
128 devices in a mesh: seq: 2 (over z_lo), ctx: 8 (over y, core), exp: 8 (over z_hi, x).
Axes of the slice: x: 4, y: 4, z: 4 (z_hi: 2, z_lo: 2; z = z_hi * 2 + z_lo), core: 2. Of those that a mesh axis runs over, the one named last changes fastest.
Arguments:
- tokens: bfloat16 [2, 8192, 7168], P('seq', ('ctx', 'exp')), may hold values from -8 to 8
- routing: int32 [2, 8192, 8], P('seq', ('ctx', 'exp')), may hold values from 0 to 255, as said below
- router_weight: bfloat16 [7168, 256], replicated, may hold values from -0.0625 to 0.0625
- w_gate: bfloat16 [16, 7168, 2048], P(('seq', 'exp'), None, 'ctx'), may hold values from -0.0625 to 0.0625
- w_up: bfloat16 [16, 7168, 2048], P(('seq', 'exp'), None, 'ctx'), may hold values from -0.0625 to 0.0625
- w_down: bfloat16 [16, 2048, 7168], P(('seq', 'exp'), 'ctx'), may hold values from -0.125 to 0.125
Outputs:
- routed: bfloat16 [2, 8192, 7168], P('seq', ('ctx', 'exp'))
- balance: float32 [2, 256], P('seq')
Inputs may be any that keep to these rules, and one draw needn't show every extreme that they name: `routing`: each token names 8 different experts. The rows of one device name any one expert at least 3 and at most 5 times; in every draw one expert below 16 is named exactly 5 times by the rows of every device.
All inputs are finite; a program needn't handle non-finite values.
Results may differ from a plain program's by a relative error of at most 0.014.
Values may be sent and summed in bfloat16 or wider, within the bound.
A program may use at most 128 MiB of HBM per device.

v0:
```python
import jax
import jax.numpy as jnp
from jax import lax
from jax.sharding import PartitionSpec as P

route_scale = 2.5


def copy_for_each(array, axis):
    copies = jnp.broadcast_to(array, (lax.axis_size(axis), *array.shape))
    return lax.all_to_all(copies, axis, split_axis=0, concat_axis=0, tiled=True)


def taken_together(array, axis):
    return copy_for_each(array, axis).sum(axis=0)


def in_one(arrays, axis):
    vector, at, done = (jnp.concatenate([a.reshape(-1) for a in arrays]), 0, [])
    total = taken_together(vector, axis)
    for a in arrays:
        done.append(total[at : at + a.size].reshape(a.shape))
        at += a.size
    return tuple(done)


def project_rows(row_block, weight):
    layout = row_block.shape
    product = jnp.dot(row_block.reshape(-1, layout[-1]), weight, preferred_element_type=jnp.float32)
    return product.reshape(layout[:-1] + (weight.shape[1],))


def on_device(tokens, routing, router_weight, w_gate, w_up, w_down):
    token_rows = tokens[0]
    routes = routing[0]
    token_count, feature_count = token_rows.shape
    top_count = routes.shape[1]
    experts = router_weight.shape[1]
    seq_count = lax.axis_size("seq")
    ctx_count = lax.axis_size("ctx")
    exp_count = lax.axis_size("exp")
    flight = seq_count * exp_count
    mean_load = token_count * top_count // experts
    capacity = mean_load + mean_load // 4
    length = token_count * ctx_count * exp_count
    logits = jnp.dot(token_rows, router_weight, preferred_element_type=jnp.float32)
    scores = jax.nn.sigmoid(logits)
    affinity = scores / jnp.sum(scores, axis=1, keepdims=True)
    picked = jnp.take_along_axis(scores, routes, axis=1)
    gate_weights = picked / jnp.sum(picked, axis=1, keepdims=True) * route_scale
    expert_iota = lax.broadcasted_iota(jnp.int32, (1, 1, experts), 2)
    load_part = jnp.sum((routes[:, :, None] == expert_iota).astype(jnp.float32), axis=(0, 1))
    prob_part = jnp.sum(affinity, axis=0)
    prob_sum, load_sum = in_one((prob_part, load_part), ("ctx", "exp"))
    balance = load_sum * (experts / (top_count * length)) * (prob_sum / length) * experts
    assignments = routes.reshape(-1)
    flight_iota = lax.broadcasted_iota(jnp.int32, (1, flight), 1)
    onehot = (assignments[:, None] == flight_iota).astype(jnp.int32)
    slot_rank = jnp.sum((jnp.cumsum(onehot, axis=0) - onehot) * onehot, axis=1)
    is_live = assignments < flight
    slot_index = jnp.where(is_live, assignments * capacity + slot_rank, flight * capacity)
    slot_iota = lax.broadcasted_iota(jnp.int32, (1, flight * capacity), 1)
    matches = slot_index[:, None] == slot_iota
    owner_iota = lax.broadcasted_iota(jnp.int32, (assignments.shape[0], 1), 0) // top_count
    source_row = jnp.sum(jnp.where(matches, owner_iota, 0), axis=0)
    filled = jnp.any(matches, axis=0)
    outgoing = jnp.where(filled[:, None], token_rows[source_row], jnp.zeros((), jnp.bfloat16))
    outgoing = outgoing.reshape(flight, capacity, feature_count)
    row_block = lax.all_gather(
        lax.all_to_all(outgoing, ("seq", "exp"), split_axis=0, concat_axis=0, tiled=True),
        "ctx",
        axis=0,
        tiled=True,
    )
    gate_proj = project_rows(row_block, w_gate[0])
    up_proj = project_rows(row_block, w_up[0])
    hidden = (jax.nn.silu(gate_proj) * up_proj).astype(jnp.bfloat16)
    summed = lax.psum_scatter(
        project_rows(hidden, w_down[0]).astype(jnp.bfloat16), "ctx", scatter_dimension=0, tiled=True
    )
    returned = lax.all_to_all(summed, ("seq", "exp"), split_axis=0, concat_axis=0, tiled=True)
    returned = returned.reshape(flight * capacity, feature_count)
    live_gates = jnp.where(is_live.reshape(token_count, top_count), gate_weights, 0.0)
    row_index = jnp.where(is_live, slot_index, 0).reshape(token_count, top_count)
    combined = jnp.zeros((token_count, feature_count), jnp.float32)
    for column in range(top_count):
        combined = combined + live_gates[:, column : column + 1] * returned[row_index[:, column]]
    return (combined.astype(jnp.bfloat16)[None], balance[None])


def solution(mesh):
    placed = (
        P("seq", ("ctx", "exp"), None),
        P("seq", ("ctx", "exp"), None),
        P(),
        P(("seq", "exp"), None, "ctx"),
        P(("seq", "exp"), None, "ctx"),
        P(("seq", "exp"), "ctx", None),
    )
    return jax.shard_map(
        on_device,
        mesh=mesh,
        in_specs=placed,
        out_specs=(P("seq", ("ctx", "exp"), None), P("seq", None)),
        check_vma=False,
    )
```

profile of v0, /device:TPU:1, one launch (start us, length us, event | category | flops | bytes accessed | tf_op | source)
XLA Modules:
  0.0 254.6 jit_solution(14456424941940430869)
XLA Ops:
  7.2 0.0 copy-start
  7.2 0.0 all-gather.2.cloned.1.call-start
  7.2 0.9 copy.46
  8.1 0.1 reshape_squeeze.6
  8.2 0.1 eq.52
  8.3 4.5 %reduce-window.6 = s32[16,8,128]{2,1,0:T(8,128)S(1)} reduce-window(s32[16,8,128]{2,1,0:T(8,128)S(1)} %fusion.34, s32[]{:T(128)} %constant.22.clone.1), window={size=1x1x128 pad=0_0x0_0x127_0}, to_apply=%region_1.0 | reduce-window | flops 2080768 | bytes 131076 | tf_op jit(solution)/shard_map/reduce-window
  12.9 0.1 slice.101
  12.9 0.1 copy.50
  13.1 0.1 copy.51
  13.2 0.1 broadcast_add_fusion
  13.3 0.1 fusion.21
  13.5 0.1 select_reduce_fusion
  13.6 0.1 broadcast_in_dim.64
  13.7 0.0 copy-done
  13.7 1.3 gather_fusion
  15.0 1.5 gather.35
  16.5 1.7 broadcast_select_fusion
  18.2 32.9 %all_to_all.16 = bf16[16,5,7168]{2,1,0:T(8,128)(2,1)S(1)} all-to-all(bf16[16,5,7168]{2,1,0:T(8,128)(2,1)S(1)} %broadcast_select_fusion), channel_id=1, replica_groups=mesh['seq'=2,'ctx'=8,'exp'=8] {'seq','exp'}, dimensions={0} | all-to-all | bytes 2293760 | tf_op jit(solution)/shard_map/all_to_all | solution.py:70
  51.1 1.8 copy.52
  52.9 0.0 all-gather.2.cloned.1.call-update
  52.9 0.0 reduce-scatter.2.cloned.1.call-start
  53.0 52.1 %all-gather.2.cloned.1.call-done = bf16[128,5,7168]{2,0,1:T(8,128)(2,1)} async-done(((bf16[16,5,7168]{2,0,1:T(8,128)(2,1)}), bf16[128,5,7168]{2,0,1:T(8,128)(2,1)}) %all-gather.2.cloned.1.call-update) | async-done | bytes 9175056 | tf_op jit(solution)/shard_map/all_gather | solution.py:69
  105.1 0.0 copy-start.4
  105.1 7.3 %fusion.11 = f32[128,5,256]{2,0,1:T(8,128)S(1)} fusion(bf16[128,5,7168]{2,0,1:T(8,128)(2,1)} %all-gather.2.cloned.1.call-done, bf16[1,7168,256]{2,1,0:T(8,128)(2,1)} %param.9), kind=kOutput, calls=%fused_computation.30 | convolution fusion | flops 2348810240 | bytes 13500416 | tf_op jit(solution)/shard_map/dot_general | solution.py:29
  112.4 0.0 copy-done.4
  112.4 1.0 copy-done.5
  113.4 2.5 fusion.16
  115.9 0.0 copy-done.2
  115.9 6.1 %convolution_convert_fusion = bf16[128,5,7168]{2,0,1:T(8,128)(2,1)} fusion(bf16[128,5,256]{2,0,1:T(8,128)(2,1)S(1)} %fusion.16, bf16[1,256,7168]{2,1,0:T(8,128)(2,1)S(1)} %copy-done.2), kind=kOutput, calls=%fused_computation.10 | convolution fusion | flops 2353397760 | bytes 13172736 | tf_op jit(solution)/shard_map/dot_general | solution.py:29
  122.0 0.0 reduce-scatter.2.cloned.1.call-update
  122.0 0.0 copy-start.3
  122.0 2.8 %fusion.44 = (f32[128]{0:T(128)S(1)}, f32[128,256]{1,0:T(8,128)S(1)}, f32[128,256]{1,0:T(8,128)S(1)}) fusion(bf16[7168,256]{1,0:T(8,128)(2,1)} %param.8, bf16[1,128,7168]{2,1,0:T(8,128)(2,1)S(1)} %copy-done), kind=kOutput, calls=%fused_computation.110 | convolution fusion | flops 469892992 | bytes 5767680 | tf_op jit(solution)/shard_map/dot_general | solution.py:46
  124.8 0.1 fusion.22
  124.9 0.2 convert_reduce_fusion
  125.2 0.7 broadcast_in_dim.70
  125.9 9.0 %all-to-all-start.2 = ((f32[64,1,512]{2,1,0:T(1,128)}), f32[64,1,512]{2,1,0:T(1,128)S(1)}, u32[]{:S(2)}, u32[]{:S(2)}) async-start(f32[64,1,512]{2,1,0:T(1,128)} %broadcast_in_dim.70), calls=%async_computation.3 | async-start | bytes 262144 | tf_op jit(solution)/shard_map/all_to_all | solution.py:11
  134.9 0.1 reduce_sum.71
  135.0 0.0 copy-done.3
  135.1 0.4 fusion.23
  135.4 43.6 %reduce-scatter.2.cloned.1.call-done = bf16[16,5,7168]{2,0,1:T(8,128)(2,1)} async-done(((bf16[128,5,7168]{2,0,1:T(8,128)(2,1)}), bf16[16,5,7168]{2,0,1:T(8,128)(2,1)}) %reduce-scatter.2.cloned.1.call-update) | async-done | bytes 1146896 | tf_op jit(solution)/shard_map/reduce_scatter | solution.py:78
  179.0 3.2 %copy.53 = bf16[16,5,7168]{2,1,0:T(8,128)(2,1)} copy(bf16[16,5,7168]{2,0,1:T(8,128)(2,1)} %reduce-scatter.2.cloned.1.call-done) | data formatting | bytes 2293760 | tf_op jit(solution)/shard_map/reduce_scatter | solution.py:78
  182.2 0.0 all-to-all-done.2
  182.2 6.7 %all-to-all-start.1 = ((bf16[16,5,7168]{2,1,0:T(8,128)(2,1)}), bf16[16,5,7168]{2,1,0:T(8,128)(2,1)}, u32[]{:S(2)}, u32[]{:S(2)}) async-start(bf16[16,5,7168]{2,1,0:T(8,128)(2,1)} %copy.53), calls=%async_computation.2 | async-start | bytes 3670016 | tf_op jit(solution)/shard_map/all_to_all | solution.py:81
  188.9 0.1 copy.47
  189.0 0.1 reshape.581
  189.1 8.6 %gather_fusion.9 = f32[1024]{0:T(1024)S(1)} fusion(f32[128,256]{1,0:T(8,128)S(1)} %get-tuple-element.19, s32[1024]{0:T(1024)S(1)} %reshape.581), kind=kCustom, calls=%fused_computation.9 | custom fusion | bytes 16384 | tf_op jit(solution)/shard_map/jit(take_along_axis)/gather | solution.py:49
  197.7 0.1 reshape.584
  197.8 0.1 fusion.35
  197.9 0.1 multiply_select_fusion
  198.0 0.4 slice_reduce_fusion.7
  198.4 0.1 reduce_sum.75
  198.5 0.6 multiply_multiply_fusion
  199.1 15.1 %all-to-all-done.1 = bf16[16,5,7168]{2,1,0:T(8,128)(2,1)} async-done(((bf16[16,5,7168]{2,1,0:T(8,128)(2,1)}), bf16[16,5,7168]{2,1,0:T(8,128)(2,1)}, u32[]{:S(2)}, u32[]{:S(2)}) %all-to-all-start.1) | async-done | bytes 1146912 | tf_op jit(solution)/shard_map/all_to_all | solution.py:81
  214.2 1.7 reshape.500
  216.0 2.9 %gather_fusion.8 = bf16[128,7168]{1,0:T(8,128)(2,1)} fusion(bf16[80,7168]{1,0:T(8,128)(2,1)S(1)} %reshape.500, s32[1024]{0:T(1024)S(1)} %get-tuple-element.23), kind=kCustom, calls=%fused_computation.8 | custom fusion | bytes 3670528 | tf_op jit(solution)/shard_map/gather | solution.py:87
  218.9 3.0 %gather_fusion.7 = bf16[128,7168]{1,0:T(8,128)(2,1)} fusion(bf16[80,7168]{1,0:T(8,128)(2,1)S(1)} %reshape.500, s32[1024]{0:T(1024)S(1)} %get-tuple-element.24), kind=kCustom, calls=%fused_computation.7 | custom fusion | bytes 3670528 | tf_op jit(solution)/shard_map/gather | solution.py:87
  221.9 2.9 %gather_fusion.6 = bf16[128,7168]{1,0:T(8,128)(2,1)} fusion(bf16[80,7168]{1,0:T(8,128)(2,1)S(1)} %reshape.500, s32[1024]{0:T(1024)S(1)} %get-tuple-element.25), kind=kCustom, calls=%fused_computation.6 | custom fusion | bytes 3670528 | tf_op jit(solution)/shard_map/gather | solution.py:87
  224.8 3.0 %gather_fusion.5 = bf16[128,7168]{1,0:T(8,128)(2,1)} fusion(bf16[80,7168]{1,0:T(8,128)(2,1)S(1)} %reshape.500, s32[1024]{0:T(1024)S(1)} %get-tuple-element.26), kind=kCustom, calls=%fused_computation.5 | custom fusion | bytes 3670528 | tf_op jit(solution)/shard_map/gather | solution.py:87
  227.8 3.0 %gather_fusion.4 = bf16[128,7168]{1,0:T(8,128)(2,1)} fusion(bf16[80,7168]{1,0:T(8,128)(2,1)S(1)} %reshape.500, s32[1024]{0:T(1024)S(1)} %get-tuple-element.27), kind=kCustom, calls=%fused_computation.4 | custom fusion | bytes 3670528 | tf_op jit(solution)/shard_map/gather | solution.py:87
  230.7 3.0 %gather_fusion.3 = bf16[128,7168]{1,0:T(8,128)(2,1)} fusion(bf16[80,7168]{1,0:T(8,128)(2,1)S(1)} %reshape.500, s32[1024]{0:T(1024)S(1)} %get-tuple-element.28), kind=kCustom, calls=%fused_computation.3 | custom fusion | bytes 3670528 | tf_op jit(solution)/shard_map/gather | solution.py:87
  233.8 3.0 %gather_fusion.2 = bf16[128,7168]{1,0:T(8,128)(2,1)} fusion(bf16[80,7168]{1,0:T(8,128)(2,1)S(1)} %reshape.500, s32[1024]{0:T(1024)S(1)} %get-tuple-element.29), kind=kCustom, calls=%fused_computation.2 | custom fusion | bytes 3670528 | tf_op jit(solution)/shard_map/gather | solution.py:87
  236.7 2.9 %gather_fusion.1 = bf16[128,7168]{1,0:T(8,128)(2,1)} fusion(bf16[80,7168]{1,0:T(8,128)(2,1)S(1)} %reshape.500, s32[1024]{0:T(1024)S(1)} %get-tuple-element.30), kind=kCustom, calls=%fused_computation.1 | custom fusion | bytes 3670528 | tf_op jit(solution)/shard_map/gather | solution.py:87
  239.7 8.1 %fusion.1 = bf16[1,128,7168]{2,1,0:T(8,128)(2,1)} fusion(bf16[128,7168]{1,0:T(8,128)(2,1)} %gather_fusion.8, bf16[128,7168]{1,0:T(8,128)(2,1)} %gather_fusion.7, bf16[128,7168]{1,0:T(8,128)(2,1)} %gather_fusion.6, bf16[128,7168]{1,0:T(8,128)(2,1)} %gather_fusion.5, bf16[128,7168]{1,0:T(8,128)(2,1)} %gather_fusion.4, bf16[128,7168]{1,0:T(8,128)(2,1)} %gather_fusion.3, ...), kind=kLoop, calls=%fused_computation.13 | loop fusion | flops 22020096 | bytes 16519168 | tf_op jit(solution)/shard_map/convert_element_type | solution.py:88
  247.8 0.0 copy-done.1
  (17 shorter events, 0.2 us)
Async XLA Ops:
  7.2 6.5 %copy-start = (bf16[1,128,7168]{2,1,0:T(8,128)(2,1)S(1)}, bf16[1,128,7168]{2,1,0:T(8,128)(2,1)}, u32[]{:S(2)}) copy-start(bf16[1,128,7168]{2,1,0:T(8,128)(2,1)} %param.6) | copy-start | bytes 5505028
  7.2 97.9 %all-gather.2.cloned.1.call-start = ((), (), s32[]{:S(2)}) async-start(), calls=%async_computation.4 | async-start | bytes 10321920 | tf_op jit(solution)/shard_map/all_gather | solution.py:69
  52.9 126.1 %reduce-scatter.2.cloned.1.call-start = ((), (), s32[]{:S(2)}) async-start(), calls=%async_computation.5 | async-start | bytes 10321920 | tf_op jit(solution)/shard_map/reduce_scatter | solution.py:78
  105.1 7.3 %copy-start.4 = (bf16[128,5,7168]{2,0,1:T(8,128)(2,1)S(1)}, bf16[128,5,7168]{2,0,1:T(8,128)(2,1)}, u32[]{:S(2)}) copy-start(bf16[128,5,7168]{2,0,1:T(8,128)(2,1)} %all-gather.2.cloned.1.call-done) | copy-start | bytes 27525124
  105.1 8.3 %copy-start.5 = (bf16[1,7168,256]{2,1,0:T(8,128)(2,1)S(1)}, bf16[1,7168,256]{2,1,0:T(8,128)(2,1)}, u32[]{:S(2)}) copy-start(bf16[1,7168,256]{2,1,0:T(8,128)(2,1)} %param.10) | copy-start | bytes 11010052
  113.4 2.5 copy-start.2
  122.0 13.0 %copy-start.3 = (s32[1,128,8]{1,2,0:T(8,128)S(1)}, s32[1,128,8]{1,2,0:T(8,128)}, u32[]{:S(2)}) copy-start(s32[1,128,8]{1,2,0:T(8,128)} %param.7) | copy-start | bytes 12292
  125.9 56.3 %all-to-all-start.2 = ((f32[64,1,512]{2,1,0:T(1,128)}), f32[64,1,512]{2,1,0:T(1,128)S(1)}, u32[]{:S(2)}, u32[]{:S(2)}) async-start(f32[64,1,512]{2,1,0:T(1,128)} %broadcast_in_dim.70), calls=%async_computation.3 | async-start | bytes 262144 | tf_op jit(solution)/shard_map/all_to_all | solution.py:11
  182.2 32.1 %all-to-all-start.1 = ((bf16[16,5,7168]{2,1,0:T(8,128)(2,1)}), bf16[16,5,7168]{2,1,0:T(8,128)(2,1)}, u32[]{:S(2)}, u32[]{:S(2)}) async-start(bf16[16,5,7168]{2,1,0:T(8,128)(2,1)} %copy.53), calls=%async_computation.2 | async-start | bytes 3670016 | tf_op jit(solution)/shard_map/all_to_all | solution.py:81
  239.7 8.1 %copy-start.1 = (bf16[1,128,7168]{2,1,0:T(8,128)(2,1)S(1)}, bf16[1,128,7168]{2,1,0:T(8,128)(2,1)}, u32[]{:S(2)}) copy-start(bf16[1,128,7168]{2,1,0:T(8,128)(2,1)} %param.6) | copy-start | bytes 5505028
Sparse Core Ops, SparseCore 0:
  53.1 51.9 all-gather.1
  122.1 56.8 reduce-scatter.1
where the time goes:
time: 259 us; the launch traced here: 255 us
  waiting for transfers between devices  111 us (43%)
  local copies, waits for them, and re-layouts  45.6 us (18%)
  blocking collectives  32.9 us (13%)
  matrix products  18.7 us (7%)
  other arithmetic  16.4 us (6%)
  starting transfers between devices  15.8 us (6%)
  between operations  14.3 us (6%)
    all_gather x1, waiting for transfers between devices, on_device(): lax.all_gather(lax.all_to_all(outgoing, ('seq', 'exp'), split_axis=0, con...  52.1 us
    reduce_scatter x1, waiting for transfers between devices, on_device(): lax.psum_scatter(project_rows(hidden, w_down[0]).astype(jnp.bfloat16), 'c...  43.6 us
    all_to_all x1, blocking collectives, on_device(): lax.all_to_all(outgoing, ('seq', 'exp'), split_axis=0, concat_axis=0, til...  32.9 us
    gather x8, local copies, waits for them, and re-layouts, on_device(): returned[row_index[:, column]]  23.7 us
    dot_general x3, matrix products, project_rows(): jnp.dot(row_block.reshape(-1, layout[-1]), weight, preferred_element_type...  15.9 us
    all_to_all x1, waiting for transfers between devices, on_device(): lax.all_to_all(summed, ('seq', 'exp'), split_axis=0, concat_axis=0, tiled...  15.1 us
    all_to_all x1, starting transfers between devices, copy_for_each(): return lax.all_to_all(copies, axis, split_axis=0, concat_axis=0, tiled=True)  9.05 us
    gather x4, local copies, waits for them, and re-layouts, on_device(): picked = jnp.take_along_axis(scores, routes, axis=1)  8.86 us
  transfers between devices with their start and end apart: 4, of which 3 were waited for; matrix products, arithmetic and copies ran while one was open for 7% of the time, Pallas kernels for 0%

commit v1 on v0

v1 whole, which is shorter than its diff:
```python
import jax
import jax.numpy as jnp
from jax import lax
from jax.experimental import pallas as pl
from jax.experimental.pallas import tpu as pltpu
from jax.sharding import PartitionSpec as P

MESH = pl.DeviceIdType.MESH
F32 = jnp.float32
BF16 = jnp.bfloat16

TOKS = 128
D = 7168
EXPERTS = 256
TOP = 8
FLIGHT = 16
CAP = 5
PAD = 8
HID = 256
ROWS = FLIGHT * CAP
LENGTH = 8192
HALF = D // 2

NC, C = 7, 1024
NM, CM = 7, 512
LEAD = 2


def dot(a, b):
    return jnp.dot(a, b, preferred_element_type=F32)


def iota(shape, dim):
    return lax.broadcasted_iota(jnp.int32, shape, dim)


def kernel(
    tok_h, routes_ref, rw_h, wg_h, wu_h, wd_h,
    out_h, bal_ref,
    tok, rw, wg, wu, wd, disp, sel, exd, ghi, glo, logits,
    asend, arecv, xb, accg, accu, hb,
    t3, t2, t1, s1, s2, f1, f2, rsend, rrecv, outb,
    sta, str_, stb,
    load_sem, out_sem, wdx_sem, a_send, a_recv, g_send, g1, g2, g3a, g3b, gd,
    h_sem, b_send, b_s1, b_s2, b_f1, b_f2, r_send, r_recv, sta_send, sta_recv, stb_send, stb_recv,
):
    s = lax.axis_index("seq")
    cx = lax.axis_index("ctx")
    ex = lax.axis_index("exp")
    core = lax.rem(cx, 2)
    other = 1 - core
    y = lax.div(cx, 2)
    zh = lax.div(ex, 4)
    xx = lax.rem(ex, 4)
    me = s * 8 + ex

    def at_y(step, which=None):
        return (s, lax.rem(y + step, 4) * 2 + (core if which is None else which), ex)

    up, down, far = at_y(1), at_y(3), at_y(2)
    peer = (s, y * 2 + other, ex)

    plane = []
    for dx in range(4):
        for dh in range(2):
            for dl in range(2):
                ps = lax.rem(s + dl, 2)
                pe = lax.rem(zh + dh, 2) * 4 + lax.rem(xx + dx, 4)
                plane.append((ps, pe, ps * 8 + pe))

    def rcopy(src, dst, ssem, rsem, dev):
        return pltpu.make_async_remote_copy(
            src_ref=src, dst_ref=dst, send_sem=ssem, recv_sem=rsem, device_id=dev, device_id_type=MESH
        )

    def load(src, dst, k):
        return pltpu.make_async_copy(src, dst, load_sem.at[k])

    mine = pl.ds(pl.multiple_of(core * HALF, 128), HALF)
    theirs = pl.ds(pl.multiple_of(other * HALF, 128), HALF)
    loads = [
        load(tok_h, tok, 0),
        load(rw_h, rw, 1),
        load(wg_h, wg, 2),
        load(wu_h, wu, 3),
        load(wd_h.at[:, mine], wd.at[core], 4),
    ]
    for cp in loads:
        cp.start()

    barrier = pltpu.get_barrier_semaphore()
    friends = [(ps, y * 2 + core, pe) for ps, pe, _ in plane[1:]]
    friends += [(ps, y * 2 + other, pe) for ps, pe, _ in plane]
    friends += [up, down, far]
    for dev in friends:
        pl.semaphore_signal(barrier, inc=1, device_id=dev, device_id_type=MESH)

    routes = routes_ref[...]
    lane = iota((TOKS, TOKS), 1)
    sub = iota((TOKS, TOKS), 0)
    hit = jnp.zeros((TOKS, TOKS), F32)
    for k in range(TOP):
        hit = hit + jnp.where(routes[:, k : k + 1] == (lane >> 3), 1.0, 0.0)
    before = jnp.where(lane < sub, 1.0, 0.0).astype(BF16)
    rank = dot(before, hit.astype(BF16))
    place = jnp.where(rank == (lane & 7).astype(F32), hit, 0.0)
    ghi[...] = place.astype(BF16)
    disp[...] = place.T.astype(BF16)
    si, sl = iota((ROWS, TOKS), 0), iota((ROWS, TOKS), 1)
    sel[...] = jnp.where((si == (sl >> 3) * CAP + (sl & 7)) & ((sl & 7) < CAP), 1.0, 0.0).astype(BF16)
    ei, el = iota((TOKS, ROWS), 1), iota((TOKS, ROWS), 0)
    exd[...] = jnp.where((ei == (el >> 3) * CAP + (el & 7)) & ((el & 7) < CAP), 1.0, 0.0).astype(BF16)
    logits[...] = jnp.zeros_like(logits)
    accg[...] = jnp.zeros_like(accg)
    accu[...] = jnp.zeros_like(accu)

    pl.semaphore_wait(barrier, len(friends))
    wdx = rcopy(wd_h.at[:, theirs], wd.at[core], wdx_sem.at[0], wdx_sem.at[1], peer)
    wdx.start()
    loads[0].wait()

    def a_copy(j, i):
        ps, pe, pm = plane[i]
        return rcopy(asend.at[j, pm], arecv.at[j, me], a_send.at[j], a_recv.at[j], (ps, cx, pe))

    def dispatch(j, carry):
        cols = pl.ds(pl.multiple_of(j * C, 128), C)
        rows = dot(disp[...], tok[:, cols])
        asend[j] = rows.reshape(FLIGHT, PAD, C).astype(BF16)
        for i in range(1, 16):
            a_copy(j, i).start()
        arecv[j, me] = asend[j, me]
        return carry

    lax.fori_loop(0, NC, dispatch, 0)
    for cp in loads[1:4]:
        cp.wait()

    def a_wait(j):
        w = rcopy(asend.at[j, pl.ds(0, 15)], arecv.at[j, pl.ds(0, 15)], a_send.at[j], a_recv.at[j], peer)
        w.wait_recv()

    hc = C // 2

    def g_own_up(j):
        return rcopy(xb.at[j, core], xb.at[j, 2 + core], g_send.at[0, j], g1.at[j], up)

    def g_own_down(j):
        return rcopy(xb.at[j, core], xb.at[j, 4 + core], g_send.at[1, j], g2.at[j], down)

    def g_far_up(j):
        return rcopy(
            xb.at[j, 2 + core, :, pl.ds(0, hc)], xb.at[j, 6 + core, :, pl.ds(0, hc)], g_send.at[2, j], g3a.at[j], up
        )

    def g_far_down(j):
        return rcopy(
            xb.at[j, 4 + core, :, pl.ds(hc, hc)], xb.at[j, 6 + core, :, pl.ds(hc, hc)], g_send.at[3, j], g3b.at[j], down
        )

    def g_peer(j, rel):
        return rcopy(
            xb.at[j, 2 * rel + core], xb.at[j, 2 * rel + core], g_send.at[4 + rel, j], gd.at[rel, j], peer
        )

    def g_peer_wait(j, rel):
        rcopy(
            xb.at[j, 2 * rel + core], xb.at[j, 2 * rel + other], g_send.at[4 + rel, j], gd.at[rel, j], peer
        ).wait_recv()

    def gather(i, carry):
        @pl.when(i < NC)
        def _():
            j = i
            a_wait(j)
            got = arecv[j].astype(F32).reshape(TOKS, C).astype(BF16)
            xb[j, core] = dot(sel[...], got).astype(BF16)
            g_own_up(j).start()
            g_own_down(j).start()
            g_peer(j, 0).start()
            cols = pl.ds(pl.multiple_of(j * C, 128), C)
            logits[...] += dot(tok[:, cols], rw[cols, :])

        @pl.when(i >= 3)
        def _():
            j = i - 3
            for rel in range(4):
                g_peer_wait(j, rel)
            rows = pl.ds(pl.multiple_of(j * C, 128), C)
            for rel in range(4):
                at = slice(rel * 2 * ROWS, (rel + 1) * 2 * ROWS)
                v = xb[j, 2 * rel : 2 * rel + 2].reshape(2 * ROWS, C)
                accg[at, :] += dot(v, wg[rows, :])
                accu[at, :] += dot(v, wu[rows, :])

        @pl.when((i >= 1) & (i < NC + 1))
        def _():
            j = i - 1
            g_own_up(j).wait_recv()
            g_far_up(j).start()
            g_peer(j, 1).start()
            g_own_down(j).wait_recv()
            g_far_down(j).start()
            g_peer(j, 2).start()

        @pl.when((i >= 2) & (i < NC + 2))
        def _():
            j = i - 2
            g_far_up(j).wait_recv()
            g_far_down(j).wait_recv()
            g_peer(j, 3).start()

        return carry

    lax.fori_loop(0, NC + 3, gather, 0)

    gate = accg[...]
    hb[core] = (gate * jax.nn.sigmoid(gate) * accu[...]).astype(BF16)
    hx = rcopy(hb.at[core], hb.at[core], h_sem.at[0], h_sem.at[1], peer)
    hx.start()
    loads[4].wait()
    wdx.wait_recv()
    rcopy(hb.at[core], hb.at[other], h_sem.at[0], h_sem.at[1], peer).wait_recv()

    hm = CM // 2

    def down_rows(rel, cols):
        at = slice(rel * 2 * ROWS, (rel + 1) * 2 * ROWS)
        return dot(hb[0, at, :], wd[0, :, cols]) + dot(hb[1, at, :], wd[1, :, cols])

    def b_far_up(m):
        return rcopy(t3.at[m, 0], s1.at[m], b_send.at[0, m], b_s1.at[m], up)

    def b_far_down(m):
        return rcopy(t3.at[m, 1], s2.at[m], b_send.at[1, m], b_s2.at[m], down)

    def b_up(m):
        return rcopy(t2.at[m], f1.at[m], b_send.at[2, m], b_f1.at[m], up)

    def b_down(m):
        return rcopy(t1.at[m], f2.at[m], b_send.at[3, m], b_f2.at[m], down)

    def r_copy(m, rel, i):
        ps, pe, pm = plane[i]
        cc = core if rel == 0 else other
        return rcopy(
            rsend.at[m, cc, pm], rrecv.at[core * NM + m, me], r_send.at[rel, m], r_recv.at[core * NM + m], (ps, y * 2 + cc, pe)
        )

    def out_copy(half, m):
        cols = pl.ds(pl.multiple_of(half * HALF + m * CM, 128), CM)
        return pltpu.make_async_copy(outb.at[:, cols], out_h.at[:, cols], out_sem.at[half, m])

    def st_a(i, rel):
        ps, pe, pm = plane[i]
        cc = core if rel == 0 else other
        return rcopy(sta.at[0], str_.at[core * 16 + me], sta_send, sta_recv, (ps, y * 2 + cc, pe))

    def st_b(dev):
        return rcopy(sta.at[1], stb.at[y], stb_send, stb_recv, dev)

    def statistics():
        scores = jax.nn.sigmoid(logits[...])
        eye = iota((TOKS, EXPERTS), 1)
        named = jnp.zeros((TOKS, EXPERTS), F32)
        for k in range(TOP):
            named = named + jnp.where(routes_ref[:, k : k + 1] == eye, 1.0, 0.0)
        affinity = scores / jnp.sum(scores, axis=1, keepdims=True)
        sta[0, 0:1, :] = jnp.sum(affinity, axis=0, keepdims=True)
        sta[0, 1:2, :] = jnp.sum(named, axis=0, keepdims=True)
        total = jnp.sum(jnp.where(named > 0.0, scores, 0.0), axis=1, keepdims=True)
        weights = scores / total * 2.5
        spread = jnp.where(iota((EXPERTS, TOKS), 0) == (iota((EXPERTS, TOKS), 1) >> 3), 1.0, 0.0)
        wide = jnp.dot(weights, spread, preferred_element_type=F32, precision=lax.Precision.HIGHEST)
        g = jnp.where(ghi[...].astype(F32) > 0.0, wide, 0.0)
        hi = g.astype(BF16)
        ghi[...] = hi
        glo[...] = (g - hi.astype(F32)).astype(BF16)
        for rel in range(2):
            for i in range(16):
                if plane_same_seq(i) and (rel, i) != (0, 0):
                    st_a(i, rel).start()

    def plane_same_seq(i):
        return i % 2 == 0

    def statistics_next():
        rcopy(str_.at[pl.ds(0, 15)], str_.at[pl.ds(0, 15)], sta_send, sta_recv, peer).wait_recv()
        str_[core * 16 + me] = sta[0]
        acc = jnp.zeros((2, EXPERTS), F32)
        for cc in range(2):
            for e in range(8):
                acc = acc + str_[cc * 16 + s * 8 + e]
        sta[1] = acc
        stb[y] = acc
        for dev in (up, down, far):
            st_b(dev).start()

    def backward(i, carry):
        @pl.when(i < NM)
        def _():
            m = i
            cols = pl.ds(pl.multiple_of(m * CM, 128), CM)
            v = down_rows(3, cols).astype(BF16)
            t3[m, 0] = v[:, :hm]
            t3[m, 1] = v[:, hm:]
            b_far_up(m).start()
            b_far_down(m).start()

        @pl.when((i >= LEAD) & (i < NM + LEAD))
        def _():
            m = i - LEAD
            cols = pl.ds(pl.multiple_of(m * CM, 128), CM)
            v = down_rows(2, cols)
            b_far_up(m).wait_recv()
            t2[m, :, :hm] = (v[:, :hm] + s1[m].astype(F32)).astype(BF16)
            t2[m, :, hm:] = v[:, hm:].astype(BF16)
            b_up(m).start()
            v = down_rows(1, cols)
            b_far_down(m).wait_recv()
            t1[m, :, :hm] = v[:, :hm].astype(BF16)
            t1[m, :, hm:] = (v[:, hm:] + s2[m].astype(F32)).astype(BF16)
            b_down(m).start()

        @pl.when(i == LEAD)
        def _():
            statistics()

        @pl.when(i == NM)
        def _():
            statistics_next()

        @pl.when((i >= LEAD + 1) & (i < NM + LEAD + 1))
        def _():
            m = i - LEAD - 1
            cols = pl.ds(pl.multiple_of(m * CM, 128), CM)
            v = down_rows(0, cols)
            b_up(m).wait_recv()
            b_down(m).wait_recv()
            v = (v + f1[m].astype(F32) + f2[m].astype(F32)).astype(BF16)
            for cc in range(2):
                w = dot(exd[...], v[cc * ROWS : (cc + 1) * ROWS, :])
                rsend[m, cc] = w.reshape(FLIGHT, PAD, CM).astype(BF16)
            for i2 in range(16):
                for rel in range(2):
                    if (rel, i2) != (0, 0):
                        r_copy(m, rel, i2).start()
            rrecv[core * NM + m, me] = rsend[m, core, me]

        @pl.when(i >= LEAD + 3)
        def _():
            m = i - LEAD - 3
            a, b = core * NM + m, other * NM + m
            rcopy(
                rrecv.at[a, pl.ds(0, 15)], rrecv.at[a, pl.ds(0, 15)], r_send.at[0, m], r_recv.at[a], peer
            ).wait_recv()
            rcopy(rrecv.at[b], rrecv.at[b], r_send.at[1, m], r_recv.at[b], peer).wait_recv()
            for half in range(2):
                v = rrecv[half * NM + m].astype(F32).reshape(TOKS, CM).astype(BF16)
                cols = pl.ds(pl.multiple_of(half * HALF + m * CM, 128), CM)
                outb[:, cols] = (dot(ghi[...], v) + dot(glo[...], v)).astype(BF16)
                out_copy(half, m).start()

        return carry

    lax.fori_loop(0, NM + LEAD + 3, backward, 0)

    rcopy(stb.at[pl.ds(0, 3)], stb.at[pl.ds(0, 3)], stb_send, stb_recv, peer).wait_recv()
    tot = stb[0] + stb[1] + stb[2] + stb[3]
    bal_ref[...] = tot[1:2, :] * (EXPERTS / (TOP * LENGTH)) * (tot[0:1, :] / LENGTH) * EXPERTS

    wdx.wait_send()
    hx.wait_send()
    rcopy(str_.at[pl.ds(0, 15)], str_.at[pl.ds(0, 15)], sta_send, sta_recv, peer).wait_send()
    rcopy(stb.at[pl.ds(0, 3)], stb.at[pl.ds(0, 3)], stb_send, stb_recv, peer).wait_send()

    def drain(j, carry):
        rcopy(asend.at[j, pl.ds(0, 15)], arecv.at[j, pl.ds(0, 15)], a_send.at[j], a_recv.at[j], peer).wait_send()
        g_own_up(j).wait_send()
        g_own_down(j).wait_send()
        g_far_up(j).wait_send()
        g_far_down(j).wait_send()
        for rel in range(4):
            g_peer(j, rel).wait_send()
        b_far_up(j).wait_send()
        b_far_down(j).wait_send()
        b_up(j).wait_send()
        b_down(j).wait_send()
        rcopy(rrecv.at[0], rrecv.at[0], r_send.at[1, j], r_recv.at[0], peer).wait_send()
        rcopy(
            rrecv.at[0, pl.ds(0, 15)], rrecv.at[0, pl.ds(0, 15)], r_send.at[0, j], r_recv.at[0], peer
        ).wait_send()
        for half in range(2):
            out_copy(half, j).wait()
        return carry

    lax.fori_loop(0, NM, drain, 0)


def on_device(tokens, routing, router_weight, w_gate, w_up, w_down):
    any_ = pl.BlockSpec(memory_space=pl.ANY)
    vmem = pl.BlockSpec(memory_space=pltpu.VMEM)
    V = pltpu.VMEM
    dma = pltpu.SemaphoreType.DMA
    out, bal = pl.pallas_call(
        kernel,
        out_shape=(
            jax.ShapeDtypeStruct((TOKS, D), BF16),
            jax.ShapeDtypeStruct((1, EXPERTS), F32),
        ),
        in_specs=[any_, vmem, any_, any_, any_, any_],
        out_specs=(any_, vmem),
        scratch_shapes=[
            V((TOKS, D), BF16),
            V((D, EXPERTS), BF16),
            V((D, HID), BF16),
            V((D, HID), BF16),
            V((2, HID, HALF), BF16),
            V((TOKS, TOKS), BF16),
            V((ROWS, TOKS), BF16),
            V((TOKS, ROWS), BF16),
            V((TOKS, TOKS), BF16),
            V((TOKS, TOKS), BF16),
            V((TOKS, EXPERTS), F32),
            V((NC, FLIGHT, PAD, C), BF16),
            V((NC, FLIGHT, PAD, C), BF16),
            V((NC, 8, ROWS, C), BF16),
            V((8 * ROWS, HID), F32),
            V((8 * ROWS, HID), F32),
            V((2, 8 * ROWS, HID), BF16),
            V((NM, 2, 2 * ROWS, CM // 2), BF16),
            V((NM, 2 * ROWS, CM), BF16),
            V((NM, 2 * ROWS, CM), BF16),
            V((NM, 2 * ROWS, CM // 2), BF16),
            V((NM, 2 * ROWS, CM // 2), BF16),
            V((NM, 2 * ROWS, CM), BF16),
            V((NM, 2 * ROWS, CM), BF16),
            V((NM, 2, FLIGHT, PAD, CM), BF16),
            V((2 * NM, FLIGHT, PAD, CM), BF16),
            V((TOKS, D), BF16),
            V((2, 2, EXPERTS), F32),
            V((32, 2, EXPERTS), F32),
            V((4, 2, EXPERTS), F32),
            dma((5,)),
            dma((2, NM)),
            dma((2,)),
            dma((NC,)),
            dma((NC,)),
            dma((8, NC)),
            dma((NC,)),
            dma((NC,)),
            dma((NC,)),
            dma((NC,)),
            dma((4, NC)),
            dma((2,)),
            dma((4, NM)),
            dma((NM,)),
            dma((NM,)),
            dma((NM,)),
            dma((NM,)),
            dma((2, NM)),
            dma((2 * NM,)),
            dma(()),
            dma(()),
            dma(()),
            dma(()),
        ],
        compiler_params=pltpu.CompilerParams(
            collective_id=0, has_side_effects=True, vmem_limit_bytes=62 * 1024 * 1024
        ),
    )(tokens[0], routing[0], router_weight, w_gate[0], w_up[0], w_down[0])
    return out[None], bal


def solution(mesh):
    placed = (
        P("seq", ("ctx", "exp"), None),
        P("seq", ("ctx", "exp"), None),
        P(),
        P(("seq", "exp"), None, "ctx"),
        P(("seq", "exp"), None, "ctx"),
        P(("seq", "exp"), "ctx", None),
    )
    return jax.shard_map(
        on_device,
        mesh=mesh,
        in_specs=placed,
        out_specs=(P("seq", ("ctx", "exp"), None), P("seq", None)),
        check_vma=False,
    )
```

time: 259 us -> 116 us (0.45); the launches traced: 255 us -> 115 us
  waiting for transfers between devices: 111 us -> 0 us
  Pallas kernels: 0 us -> 110 us
  local copies, waits for them, and re-layouts: 45.6 us -> 4.83 us
  blocking collectives: 32.9 us -> 0 us
  matrix products: 18.7 us -> 0 us
  other arithmetic: 16.4 us -> 0 us
  starting transfers between devices: 15.8 us -> 0 us
  between operations: 14.3 us -> 0.65 us
    pallas_call x0 -> x1, Pallas kernels: none -> 110 us  [on_device(): pl.pallas_call(kernel, out_shape=(jax.ShapeDtypeStruct((TOKS, D), BF16),...]
    all_gather x1 -> x0, waiting for transfers between devices: 52.1 us -> none  [on_device(): lax.all_gather(lax.all_to_all(outgoing, ('seq', 'exp'), split_axis=0, con...]
    reduce_scatter x1 -> x0, waiting for transfers between devices: 43.6 us -> none  [on_device(): lax.psum_scatter(project_rows(hidden, w_down[0]).astype(jnp.bfloat16), 'c...]
    gather x14 -> x0, local copies, waits for them, and re-layouts: 35.3 us -> none  [the longest x8 23.7 us: on_device(): returned[row_index[:, column]]]
    all_to_all x1 -> x0, blocking collectives: 32.9 us -> none  [on_device(): lax.all_to_all(outgoing, ('seq', 'exp'), split_axis=0, concat_axis=0, til...]
    dot_general x4 -> x0, matrix products: 18.7 us -> none  [the longest x3 15.9 us: project_rows(): jnp.dot(row_block.reshape(-1, layout[-1]), weight, preferred_element_type...]
    all_to_all x2 -> x0, starting transfers between devices: 15.8 us -> none  [the longest x1 9.05 us: copy_for_each(): return lax.all_to_all(copies, axis, split_axis=0, concat_axis=0, tiled=True)]
    all_to_all x2 -> x0, waiting for transfers between devices: 15.1 us -> none  [the longest x1 15.1 us: on_device(): lax.all_to_all(summed, ('seq', 'exp'), split_axis=0, concat_axis=0, tiled...]
  transfers between devices with their start and end apart: 4 -> 0, of which waited for: 3 -> 0; matrix products, arithmetic and copies ran while one was open for 7% -> 0% of each run, Pallas kernels for 0% -> 0%
where the time goes in v1:
time: 116 us; the launch traced here: 115 us
  Pallas kernels  110 us (95%)
  local copies, waits for them, and re-layouts  4.83 us (4%)
    pallas_call x1, Pallas kernels, on_device(): pl.pallas_call(kernel, out_shape=(jax.ShapeDtypeStruct((TOKS, D), BF16),...  110 us
    unnamed x5, local copies, waits for them, and re-layouts  4.83 us

profile of v1, /device:TPU:1, one launch (start us, length us, event | category | flops | bytes accessed | tf_op | source)
XLA Modules:
  0.0 115.5 jit_solution(10196486467651443605)
XLA Ops:
  0.6 1.4 %copy.8 = s32[1,128,8]{2,1,0:T(8,128)} copy(s32[1,128,8]{1,2,0:T(8,128)} %param.7) | data formatting | bytes 8192 | tf_op args[1]
  2.0 110.0 %shard_map.77 = (bf16[128,7168]{1,0:T(8,128)(2,1)}, f32[1,256]{1,0:T(1,128)}) custom-call(bf16[128,7168]{1,0:T(8,128)(2,1)} %bitcast.10, s32[128,8]{1,0:T(8,128)} %bitcast.11, bf16[7168,256]{1,0:T(8,128)(2,1)} %rw_h.1, bf16[7168,256]{1,0:T(8,128)(2,1)} %bitcast.6, bf16[7168,256]{1,0:T(8,128)(2,1)} %bitcast.7, bf16[256,7168]{1,0:T(8,128)(2,1)} %bitcast.8), custom_call_target="tpu_custom_call" | custom-call | tf_op jit(solution)/shard_map/pallas_call | solution.py:405
  112.1 0.0 copy-start
  112.1 2.8 %copy.11 = bf16[1,128,7168]{2,1,0:T(8,128)(2,1)} copy(bf16[1,128,7168]{2,1,0:T(8,128)(2,1)} %bitcast.9) | data formatting | bytes 3670016
  114.9 0.0 copy-done
  114.9 0.6 copy.12
Async XLA Ops:
  112.1 2.9 %copy-start = (f32[1,256]{1,0:T(1,128)S(1)}, f32[1,256]{1,0:T(1,128)}, u32[]{:S(2)}) copy-start(f32[1,256]{1,0:T(1,128)} %get-tuple-element.9) | copy-start | bytes 3076

commit v2 on v1

v2 whole, which is shorter than its diff:
```python
import jax
import jax.numpy as jnp
from jax import lax
from jax.experimental import pallas as pl
from jax.experimental.pallas import tpu as pltpu
from jax.sharding import PartitionSpec as P

MESH = pl.DeviceIdType.MESH
F32 = jnp.float32
BF16 = jnp.bfloat16

TOKS = 128
D = 7168
EXPERTS = 256
TOP = 8
FLIGHT = 16
CAP = 5
PAD = 8
HID = 256
ROWS = FLIGHT * CAP
LENGTH = 8192
HALF = D // 2

NC, C = 14, 512
NM, CM = 14, 256
NR = 12
NP = NC - NR
MSG = 24
AHEAD = 4
NEAR = 3
LAG = 6
LATE = 6
FIRST = 9
LEAD = 3
SUM = 3
BACK = 9


def dot(a, b):
    return jnp.dot(a, b, preferred_element_type=F32)


def iota(shape, dim):
    return lax.broadcasted_iota(jnp.int32, shape, dim)


def stage(cond, name):
    def wrap(body):
        @pl.when(cond)
        def _():
            with jax.named_scope(name):
                body()

    return wrap


def kernel(
    tok_h, routes_ref, rw_h, wg_h, wu_h, wd_h,
    out_ref, bal_ref,
    tok, rw, wg, wu, wd, disp, sel, exd, pack, unpack, yb, ys, yr, ghi, glo, logits,
    asend, arecv, xb, accg, accu, hb,
    t3, s3, nu, nd, f1, f2, rsend, rrecv,
    sta, str_, stb,
    load_sem, wdx_sem, a_send, a_recv, g_send, g1, g3, gd,
    h_sem, b_send, b_s, b_f, r_send, r_recv, st_send, st_recv, y_send, y1, y3, ym,
):
    s = lax.axis_index("seq")
    cx = lax.axis_index("ctx")
    ex = lax.axis_index("exp")
    core = lax.rem(cx, 2)
    other = 1 - core
    y = lax.div(cx, 2)
    zh = lax.div(ex, 4)
    xx = lax.rem(ex, 4)
    me = s * 8 + ex

    def at_y(step):
        return (s, lax.rem(y + step, 4) * 2 + core, ex)

    up, down, far = at_y(1), at_y(3), at_y(2)
    peer = (s, y * 2 + other, ex)

    plane = []
    for dx in range(4):
        for dh in range(2):
            for dl in range(2):
                ps = lax.rem(s + dl, 2)
                pe = lax.rem(zh + dh, 2) * 4 + lax.rem(xx + dx, 4)
                plane.append((ps, pe, ps * 8 + pe))

    def rcopy(src, dst, ssem, rsem, dev):
        return pltpu.make_async_remote_copy(
            src_ref=src, dst_ref=dst, send_sem=ssem, recv_sem=rsem, device_id=dev, device_id_type=MESH
        )

    mine = pl.ds(pl.multiple_of(core * HALF, 128), HALF)
    theirs = pl.ds(pl.multiple_of(other * HALF, 128), HALF)
    pairs = [(tok_h, tok), (rw_h, rw), (wg_h, wg), (wu_h, wu), (wd_h.at[:, mine], wd.at[core])]
    loads = [pltpu.make_async_copy(src, dst, load_sem.at[k]) for k, (src, dst) in enumerate(pairs)]
    for cp in loads:
        cp.start()

    barrier = pltpu.get_barrier_semaphore()
    friends = [(ps, y * 2 + core, pe) for ps, pe, _ in plane[1:]]
    friends += [(ps, y * 2 + other, pe) for ps, pe, _ in plane]
    friends += [up, down, far]
    for dev in friends:
        pl.semaphore_signal(barrier, inc=1, device_id=dev, device_id_type=MESH)

    lane = iota((TOKS, TOKS), 1)
    sub = iota((TOKS, TOKS), 0)
    hit = jnp.zeros((TOKS, TOKS), F32)
    for k in range(TOP):
        hit = hit + jnp.where(routes_ref[k : k + 1, :] == (sub >> 3), 1.0, 0.0)
    before = jnp.where(sub < lane, 1.0, 0.0).astype(BF16)
    rank = dot(hit.astype(BF16), before)
    place = jnp.where(rank == (sub & 7).astype(F32), hit, 0.0)
    disp[...] = place.astype(BF16)
    ghi[...] = place.T.astype(BF16)
    si, sl = iota((ROWS, TOKS), 0), iota((ROWS, TOKS), 1)
    sel[...] = jnp.where((si == (sl >> 3) * CAP + (sl & 7)) & ((sl & 7) < CAP), 1.0, 0.0).astype(BF16)
    ei, el = iota((TOKS, ROWS), 1), iota((TOKS, ROWS), 0)
    exd[...] = jnp.where((ei == (el >> 3) * CAP + (el & 7)) & ((el & 7) < CAP), 1.0, 0.0).astype(BF16)
    logits[...] = jnp.zeros_like(logits)
    accg[...] = jnp.zeros_like(accg)
    accu[...] = jnp.zeros_like(accu)

    with jax.named_scope("w_bar"):
        pl.semaphore_wait(barrier, len(friends))
        loads[0].wait()

    def a_copy(j, i):
        ps, pe, pm = plane[i]
        return rcopy(asend.at[j, pm], arecv.at[j, me], a_send, a_recv.at[j], (ps, cx, pe))

    def dispatch(j):
        cols = pl.ds(pl.multiple_of(j * C, 128), C)
        rows = dot(disp[...], tok[:, cols])
        asend[j] = rows.reshape(FLIGHT, PAD, C).astype(BF16)
        for i in range(1, 16):
            a_copy(j, i).start()
        arecv[j, me] = asend[j, me]

    def dispatch_first(j, carry):
        with jax.named_scope("disp"):
            dispatch(j)
        return carry

    hc = C // 2
    left, right = pl.ds(0, hc), pl.ds(hc, hc)

    def y_near(p, step):
        return rcopy(yb.at[p, 0], yb.at[p, 1 if step == 1 else 2], y_send.at[0], y1.at[p], up if step == 1 else down)

    def y_far(p, step):
        half, rel, dev = (left, 1, up) if step == 1 else (right, 2, down)
        return rcopy(yb.at[p, rel, :, half], yb.at[p, 3, :, half], y_send.at[0], y3.at[p], dev)

    with jax.named_scope("pre"):
        compact = dot(sel[...], disp[...]).astype(BF16)
        for p in range(NP):
            cols = slice((NR + p) * C, (NR + p + 1) * C)
            yb[p, 0] = dot(compact, tok[:, cols]).astype(BF16)
            y_near(p, 1).start()
            y_near(p, 3).start()

    lax.fori_loop(0, AHEAD, dispatch_first, 0)
    wdx = rcopy(wd_h.at[:, theirs], wd.at[core], wdx_sem.at[0], wdx_sem.at[1], peer)
    wdx.start()
    with jax.named_scope("w_wts"):
        for rel in range(4):
            q = iota((MSG * FLIGHT, ROWS), 1)
            q = ((q * 205) >> 10) * (MSG - CAP) + q + CAP * rel
            pack[rel] = jnp.where(q == iota((MSG * FLIGHT, ROWS), 0), 1.0, 0.0).astype(BF16)
            q = iota((ROWS, MSG * FLIGHT), 0)
            q = ((q * 205) >> 10) * (MSG - CAP) + q + CAP * rel
            unpack[rel] = jnp.where(q == iota((ROWS, MSG * FLIGHT), 1), 1.0, 0.0).astype(BF16)
        for cp in loads[1:4]:
            cp.wait()
    with jax.named_scope("w_y1"):
        for p in range(NP):
            two = yb.at[p, pl.ds(0, 2)]
            rcopy(two, two, y_send.at[0], y1.at[p], peer).wait_recv()
            y_far(p, 1).start()
            y_far(p, 3).start()

    def y_message(p, i):
        ps, pe, pm = plane[i]
        return rcopy(ys.at[p, pm], yr.at[p, me], y_send.at[1], ym.at[p], (ps, cx, pe))

    def y_messages():
        for p in range(NP):
            with jax.named_scope("w_y3"):
                rcopy(yb.at[p, 0], yb.at[p, 0], y_send.at[0], y3.at[p], peer).wait_recv()
            v = dot(pack[0], yb[p, 0])
            for rel in range(1, 4):
                v = v + dot(pack[rel], yb[p, rel])
            ys[p] = v.reshape(FLIGHT, MSG, C).astype(BF16)
            for i in range(1, 16):
                y_message(p, i).start()
            yr[p, me] = ys[p, me]
            cols = slice((NR + p) * C, (NR + p + 1) * C)
            logits[...] += dot(tok[:, cols], rw[cols, :])

    def y_arrived():
        for p in range(NP):
            with jax.named_scope("w_ym"):
                most = yr.at[p, pl.ds(0, 15)]
                rcopy(most, most, y_send.at[1], ym.at[p], peer).wait_recv()
            got = yr[p].astype(F32).reshape(FLIGHT * MSG, C).astype(BF16)
            for rel in range(4):
                xb[NR + p, 2 * rel + core] = dot(unpack[rel], got).astype(BF16)
                g_peer(NR + p, rel).start()

    def g_own_up(j):
        return rcopy(xb.at[j, core], xb.at[j, 2 + core], g_send.at[0], g1.at[j], up)

    def g_own_down(j):
        return rcopy(xb.at[j, core], xb.at[j, 4 + core], g_send.at[1], g1.at[j], down)

    def g_far_up(j):
        return rcopy(xb.at[j, 2 + core, :, left], xb.at[j, 6 + core, :, left], g_send.at[2], g3.at[j], up)

    def g_far_down(j):
        return rcopy(xb.at[j, 4 + core, :, right], xb.at[j, 6 + core, :, right], g_send.at[3], g3.at[j], down)

    def g_peer(j, rel):
        at = 2 * rel + core
        return rcopy(xb.at[j, at], xb.at[j, at], g_send.at[4 + rel], gd.at[rel // 3, j], peer)

    def g_peer_wait(j, rel):
        blocks = xb.at[j, pl.ds(0, 1 if rel == 3 else 3)]
        rcopy(blocks, blocks, g_send.at[4], gd.at[rel // 3, j], peer).wait_recv()

    def multiply(j, rel):
        rows = pl.ds(pl.multiple_of(j * C, 128), C)
        at = slice(rel * 2 * ROWS, (rel + 1) * 2 * ROWS)
        v = xb[j, 2 * rel : 2 * rel + 2].reshape(2 * ROWS, C)
        accg[at, :] += dot(v, wg[rows, :])
        accu[at, :] += dot(v, wu[rows, :])

    def relay(j):
        g_far_up(j).start()
        g_far_down(j).start()

    def relay_arrived(j):
        rcopy(xb.at[j, 0], xb.at[j, 0], g_send.at[0], g3.at[j], peer).wait_recv()
        g_peer(j, 3).start()

    def multiply_far(j):
        g_peer_wait(j, 3)
        multiply(j, 3)

    def gather(i, carry):
        @stage(i + AHEAD < NR, "disp")
        def _():
            dispatch(i + AHEAD)

        @stage(i < NR, "fa")
        def _():
            j = i
            with jax.named_scope("w_a"):
                rcopy(
                    asend.at[j, pl.ds(0, 15)], arecv.at[j, pl.ds(0, 15)], a_send, a_recv.at[j], peer
                ).wait_recv()
            got = arecv[j].astype(F32).reshape(TOKS, C).astype(BF16)
            xb[j, core] = dot(sel[...], got).astype(BF16)
            g_own_up(j).start()
            g_own_down(j).start()
            g_peer(j, 0).start()
            cols = pl.ds(pl.multiple_of(j * C, 128), C)
            logits[...] += dot(tok[:, cols], rw[cols, :])

        @stage((i >= LAG) & (i < NR), "ff")
        def _():
            relay(i - LAG)

        @stage((i >= NEAR) & (i < NR + NEAR), "fn")
        def _():
            j = i - NEAR
            with jax.named_scope("w_g1"):
                two = xb.at[j, pl.ds(0, 2)]
                rcopy(two, two, g_send.at[0], g1.at[j], peer).wait_recv()
            g_peer(j, 1).start()
            g_peer(j, 2).start()

        @stage(i == NR, "ff")
        def _():
            for j in range(NR - LAG, NR - NEAR + 1):
                relay(j)

        @stage(i == NR - AHEAD, "ymsg")
        def _():
            y_messages()

        @stage(i == NR + 2, "yarr")
        def _():
            y_arrived()

        @stage((i > NR) & (i < NR + NEAR), "ff")
        def _():
            relay(i - NEAR)

        @stage((i >= NEAR + 2), "fm")
        def _():
            j = i - NEAR - 2
            with jax.named_scope("w_d"):
                g_peer_wait(j, 0)
            for rel in range(3):
                multiply(j, rel)

        @stage((i >= LAG + 2) & (i < LAG + 2 + NR - LATE), "fc")
        def _():
            with jax.named_scope("w_g3"):
                relay_arrived(i - LAG - 2)

        @stage((i >= LAG + 4) & (i < LAG + 4 + NR - LATE), "fmf")
        def _():
            multiply_far(i - LAG - 4)

        @stage(i >= NR + NEAR + 2, "fmf")
        def _():
            multiply_far(i - NEAR - 2)

        return carry

    lax.fori_loop(0, NC + NEAR + 2, gather, 0)

    def hidden(lo, n, k):
        at = pl.ds(lo, n)
        gate = accg[at, :]
        hb[core, at, :] = (gate * jax.nn.sigmoid(gate) * accu[at, :]).astype(BF16)
        h_copy(lo, n, k, core).start()

    def h_copy(lo, n, k, slot):
        at = pl.ds(lo, n)
        return rcopy(hb.at[core, at, :], hb.at[slot, at, :], h_sem.at[0, k], h_sem.at[1, k], peer)

    near_rows, far_rows = 6 * ROWS, 2 * ROWS
    with jax.named_scope("hn"):
        hidden(0, near_rows, 0)
    with jax.named_scope("w_h"):
        loads[4].wait()
        wdx.wait_recv()
        h_copy(0, near_rows, 0, other).wait_recv()

    def chunk(m):
        return pl.ds(pl.multiple_of(m * CM, 128), CM)

    def down_rows(lo, n, m):
        at = slice(lo * ROWS, (lo + n) * ROWS)
        cols = chunk(m)
        return dot(hb[0, at, :], wd[0, :, cols]) + dot(hb[1, at, :], wd[1, :, cols])

    def b_up(m, k):
        return rcopy(nu.at[m, k], f1.at[m, k], b_send.at[k], b_f.at[m], up)

    def b_down(m, k):
        return rcopy(nd.at[m, k], f2.at[m, k], b_send.at[2 + k], b_f.at[m], down)

    def b_far_up(m):
        return rcopy(t3.at[0, m], s3.at[0, m], b_send.at[4], b_s.at[m], up)

    def b_far_down(m):
        return rcopy(t3.at[1, m], s3.at[1, m], b_send.at[5], b_s.at[m], down)

    def independent(m):
        nd[m, 0] = down_rows(2, 1, m).astype(BF16)
        b_down(m, 0).start()
        nu[m, 1] = down_rows(5, 1, m).astype(BF16)
        b_up(m, 1).start()

    def late(j):
        with jax.named_scope("w_g3"):
            relay_arrived(j)

    def step(q, carry):
        with jax.named_scope("ind"):
            independent(q)

        @stage(q >= 1, "late")
        def _():
            late(NR - LATE - 1 + q)

        @stage(q >= 3, "fmf")
        def _():
            multiply_far(NR - LATE - 3 + q)

        return carry

    lax.fori_loop(0, LATE + 1, step, 0)
    with jax.named_scope("fmf"):
        multiply_far(NR - 2)
        multiply_far(NR - 1)
    with jax.named_scope("hf"):
        hidden(near_rows, far_rows, 1)
    with jax.named_scope("ind"):
        for q in range(LATE + 1, FIRST):
            independent(q)
    with jax.named_scope("w_hf"):
        h_copy(near_rows, far_rows, 1, other).wait_recv()

    def r_copy(m, rel, i):
        ps, pe, pm = plane[i]
        cc = core if rel == 0 else other
        return rcopy(rsend.at[m, cc, pm], rrecv.at[m, core * 16 + me], r_send.at[rel], r_recv.at[m], (ps, y * 2 + cc, pe))

    def st_a(i, rel):
        ps, pe, pm = plane[i]
        cc = core if rel == 0 else other
        return rcopy(sta.at[0], str_.at[core * 16 + me], st_send.at[0], st_recv.at[0], (ps, y * 2 + cc, pe))

    def st_b(dev):
        return rcopy(sta.at[1], stb.at[y], st_send.at[1], st_recv.at[1], dev)

    all_a = rcopy(str_.at[pl.ds(0, 15)], str_.at[pl.ds(0, 15)], st_send.at[0], st_recv.at[0], peer)
    all_b = rcopy(stb.at[pl.ds(0, 3)], stb.at[pl.ds(0, 3)], st_send.at[1], st_recv.at[1], peer)

    def statistics():
        scores = jax.nn.sigmoid(logits[...])
        eye = iota((EXPERTS, TOKS), 0)
        named = jnp.zeros((EXPERTS, TOKS), F32)
        for k in range(TOP):
            named = named + jnp.where(routes_ref[k : k + 1, :] == eye, 1.0, 0.0)
        named = named.T
        affinity = scores / jnp.sum(scores, axis=1, keepdims=True)
        sta[0, 0:1, :] = jnp.sum(affinity, axis=0, keepdims=True)
        sta[0, 1:2, :] = jnp.sum(named, axis=0, keepdims=True)
        total = jnp.sum(jnp.where(named > 0.0, scores, 0.0), axis=1, keepdims=True)
        weights = scores / total * 2.5
        spread = jnp.where(iota((EXPERTS, TOKS), 0) == (iota((EXPERTS, TOKS), 1) >> 3), 1.0, 0.0)
        wide = jnp.dot(weights, spread, preferred_element_type=F32, precision=lax.Precision.HIGHEST)
        g = jnp.where(ghi[...].astype(F32) > 0.0, wide, 0.0)
        hi = g.astype(BF16)
        ghi[...] = hi
        glo[...] = (g - hi.astype(F32)).astype(BF16)
        for rel in range(2):
            for i in range(0, 16, 2):
                if (rel, i) != (0, 0):
                    st_a(i, rel).start()

    def statistics_next():
        all_a.wait_recv()
        str_[core * 16 + me] = sta[0]
        acc = jnp.zeros((2, EXPERTS), F32)
        for cc in range(2):
            for e in range(8):
                acc = acc + str_[cc * 16 + s * 8 + e]
        sta[1] = acc
        stb[y] = acc
        for dev in (up, down, far):
            st_b(dev).start()

    def backward(i, carry):
        @stage(i < NM, "bt")
        def _():
            m = i
            v = down_rows(6, 2, m)
            t3[0, m] = v[:ROWS].astype(BF16)
            t3[1, m] = v[ROWS:].astype(BF16)
            b_far_up(m).start()
            b_far_down(m).start()

        @stage((lax.rem(i, 2) == 1) & (i < 2 * (NM - FIRST)), "bi")
        def _():
            independent(FIRST + lax.div(i, 2))

        @stage((i >= LEAD) & (i < NM + LEAD), "bb")
        def _():
            m = i - LEAD
            v = down_rows(3, 2, m)
            with jax.named_scope("w_s"):
                rcopy(nu.at[m], nu.at[m], b_send.at[0], b_s.at[m], peer).wait_recv()
            nu[m, 0] = (v[ROWS:] + s3[0, m].astype(F32)).astype(BF16)
            b_up(m, 0).start()
            nd[m, 1] = (v[:ROWS] + s3[1, m].astype(F32)).astype(BF16)
            b_down(m, 1).start()

        @stage(i == LEAD + 2, "stat")
        def _():
            statistics()

        @stage(i == NM // 2, "stat")
        def _():
            statistics_next()

        @stage((i >= LEAD + SUM) & (i < NM + LEAD + SUM), "bc")
        def _():
            m = i - LEAD - SUM
            v = down_rows(0, 2, m)
            with jax.named_scope("w_f"):
                four = nu.at[pl.ds(0, 2)]
                rcopy(four, four, b_send.at[0], b_f.at[m], peer).wait_recv()
            for cc in range(2):
                at = slice(cc * ROWS, (cc + 1) * ROWS)
                r = (v[at] + f1[m, cc].astype(F32) + f2[m, cc].astype(F32)).astype(BF16)
                w = dot(exd[...], r)
                rsend[m, cc] = w.reshape(FLIGHT, PAD, CM).astype(BF16)
            for i2 in range(16):
                for rel in range(2):
                    if (rel, i2) != (0, 0):
                        r_copy(m, rel, i2).start()
            rrecv[m, core * 16 + me] = rsend[m, core, me]

        @stage(i >= LEAD + BACK, "br")
        def _():
            m = i - LEAD - BACK
            with jax.named_scope("w_r"):
                most = rrecv.at[m, pl.ds(0, 31)]
                rcopy(most, most, r_send.at[0], r_recv.at[m], peer).wait_recv()
            for half in range(2):
                v = rrecv[m, half * 16 : half * 16 + 16].astype(F32).reshape(TOKS, CM).astype(BF16)
                cols = pl.ds(pl.multiple_of(half * HALF + m * CM, 128), CM)
                out_ref[:, cols] = (dot(ghi[...], v) + dot(glo[...], v)).astype(BF16)

        return carry

    lax.fori_loop(0, NM + LEAD + BACK, backward, 0)

    with jax.named_scope("fin"):
        all_b.wait_recv()
        tot = stb[0] + stb[1] + stb[2] + stb[3]
        bal_ref[...] = tot[1:2, :] * (EXPERTS / (TOP * LENGTH)) * (tot[0:1, :] / LENGTH) * EXPERTS

        wdx.wait_send()
        h_copy(0, near_rows, 0, core).wait_send()
        h_copy(near_rows, far_rows, 1, core).wait_send()
        all_a.wait_send()
        all_b.wait_send()

        def left_(src, sem):
            rcopy(src, src, sem, r_recv.at[0], peer).wait_send()

        left_(asend.at[:, pl.ds(0, 15)], a_send)
        some = pl.ds(0, NR)
        left_(xb.at[some, core], g_send.at[0])
        left_(xb.at[some, core], g_send.at[1])
        left_(xb.at[some, core, :, left], g_send.at[2])
        left_(xb.at[some, core, :, left], g_send.at[3])
        left_(yb.at[:, pl.ds(0, 3)], y_send.at[0])
        left_(ys.at[:, pl.ds(0, 15)], y_send.at[1])
        for rel in range(4):
            left_(xb.at[:, core], g_send.at[4 + rel])
        for k in range(6):
            left_(t3.at[0], b_send.at[k])
        left_(rsend.at[:, 0, pl.ds(0, 15)], r_send.at[0])
        left_(rsend.at[:, 0], r_send.at[1])


def on_device(tokens, routing, router_weight, w_gate, w_up, w_down):
    hbm = pl.BlockSpec(memory_space=pltpu.HBM)
    vmem = pl.BlockSpec(memory_space=pltpu.VMEM)
    V = pltpu.VMEM
    dma = pltpu.SemaphoreType.DMA
    out, bal = pl.pallas_call(
        kernel,
        out_shape=(
            jax.ShapeDtypeStruct((TOKS, D), BF16),
            jax.ShapeDtypeStruct((1, EXPERTS), F32),
        ),
        in_specs=[hbm, vmem, hbm, hbm, hbm, hbm],
        out_specs=(vmem, vmem),
        scratch_shapes=[
            V((TOKS, D), BF16),
            V((D, EXPERTS), BF16),
            V((D, HID), BF16),
            V((D, HID), BF16),
            V((2, HID, HALF), BF16),
            V((TOKS, TOKS), BF16),
            V((ROWS, TOKS), BF16),
            V((TOKS, ROWS), BF16),
            V((4, MSG * FLIGHT, ROWS), BF16),
            V((4, ROWS, MSG * FLIGHT), BF16),
            V((NP, 4, ROWS, C), BF16),
            V((NP, FLIGHT, MSG, C), BF16),
            V((NP, FLIGHT, MSG, C), BF16),
            V((TOKS, TOKS), BF16),
            V((TOKS, TOKS), BF16),
            V((TOKS, EXPERTS), F32),
            V((NR, FLIGHT, PAD, C), BF16),
            V((NR, FLIGHT, PAD, C), BF16),
            V((NC, 8, ROWS, C), BF16),
            V((8 * ROWS, HID), F32),
            V((8 * ROWS, HID), F32),
            V((2, 8 * ROWS, HID), BF16),
            V((2, NM, ROWS, CM), BF16),
            V((2, NM, ROWS, CM), BF16),
            V((NM, 2, ROWS, CM), BF16),
            V((NM, 2, ROWS, CM), BF16),
            V((NM, 2, ROWS, CM), BF16),
            V((NM, 2, ROWS, CM), BF16),
            V((NM, 2, FLIGHT, PAD, CM), BF16),
            V((NM, 2 * FLIGHT, PAD, CM), BF16),
            V((2, 2, EXPERTS), F32),
            V((32, 2, EXPERTS), F32),
            V((4, 2, EXPERTS), F32),
            dma((5,)),
            dma((2,)),
            dma(()),
            dma((NR,)),
            dma((8,)),
            dma((NR,)),
            dma((NR,)),
            dma((2, NC)),
            dma((2, 2)),
            dma((6,)),
            dma((NM,)),
            dma((NM,)),
            dma((2,)),
            dma((NM,)),
            dma((2,)),
            dma((2,)),
            dma((2,)),
            dma((NP,)),
            dma((NP,)),
            dma((NP,)),
        ],
        compiler_params=pltpu.CompilerParams(
            collective_id=0, has_side_effects=True, vmem_limit_bytes=52 * 1024 * 1024
        ),
    )(tokens[0], routing[0].T, router_weight, w_gate[0], w_up[0], w_down[0])
    return out[None], bal


def solution(mesh):
    placed = (
        P("seq", ("ctx", "exp"), None),
        P("seq", ("ctx", "exp"), None),
        P(),
        P(("seq", "exp"), None, "ctx"),
        P(("seq", "exp"), None, "ctx"),
        P(("seq", "exp"), "ctx", None),
    )
    return jax.shard_map(
        on_device,
        mesh=mesh,
        in_specs=placed,
        out_specs=(P("seq", ("ctx", "exp"), None), P("seq", None)),
        check_vma=False,
    )
```

time: 116 us -> 103 us (0.89)
  Pallas kernels: 110 us -> 100 us
  local copies, waits for them, and re-layouts: 4.83 us -> 2.47 us
    pallas_call x1, Pallas kernels: 110 us -> 100 us  [on_device(): pl.pallas_call(kernel, out_shape=(jax.ShapeDtypeStruct((TOKS, D), BF16),...]
    unnamed x5 -> x4, local copies, waits for them, and re-layouts: 4.83 us -> 2.47 us
where the time goes in v2:
time: 103 us
  Pallas kernels  100 us (97%)
  local copies, waits for them, and re-layouts  2.47 us (2%)
    pallas_call x1, Pallas kernels, on_device(): pl.pallas_call(kernel, out_shape=(jax.ShapeDtypeStruct((TOKS, D), BF16),...  100 us
    unnamed x4, local copies, waits for them, and re-layouts  2.47 us

profile of v2, /device:TPU:1, one launch (start us, length us, event | category | flops | bytes accessed | tf_op | source)
XLA Modules:
  0.0 103.2 jit_solution(7829590103521668334)
XLA Ops:
  0.6 0.0 copy-start
  0.6 0.7 copy-done
  1.3 100.1 %shard_map.77 = (bf16[128,7168]{1,0:T(8,128)(2,1)S(1)}, f32[1,256]{1,0:T(1,128)S(1)}) custom-call(bf16[128,7168]{1,0:T(8,128)(2,1)} %bitcast.13, s32[8,128]{1,0:T(8,128)S(1)} %bitcast.9, bf16[7168,256]{1,0:T(8,128)(2,1)} %rw_h.1, bf16[7168,256]{1,0:T(8,128)(2,1)} %bitcast.10, bf16[7168,256]{1,0:T(8,128)(2,1)} %bitcast.11, bf16[256,7168]{1,0:T(8,128)(2,1)} %bitcast.12), custom_call_target="tpu_custom_call" | custom-call | tf_op jit(solution)/shard_map/pallas_call | solution.py:555
  101.4 1.2 %copy.10 = bf16[1,128,7168]{2,1,0:T(8,128)(2,1)} copy(bf16[1,128,7168]{2,1,0:T(8,128)(2,1)S(1)} %bitcast.8) | data formatting | bytes 3670016
  102.7 0.6 copy.11
Async XLA Ops:
  0.6 0.7 copy-start

commit v3 on v2

--- a/solution.py
+++ b/solution.py
@@ -26,14 +26,21 @@
 NR = 12
 NP = NC - NR
 MSG = 24
-AHEAD = 4
+AHEAD = 6
 NEAR = 3
 LAG = 6
-LATE = 6
-FIRST = 9
+FAR = 10
+EARLY = 3
+NL = 3
+NB = NM - NL
+PLACE = 8 * CAP
+FIRST = 7
 LEAD = 3
 SUM = 3
 BACK = 9
+
+
+SLOT = ((0, 1), (2, 4), (5, 3), (6, 7))
 
 
 def dot(a, b):
@@ -59,10 +66,10 @@
     out_ref, bal_ref,
     tok, rw, wg, wu, wd, disp, sel, exd, pack, unpack, yb, ys, yr, ghi, glo, logits,
     asend, arecv, xb, accg, accu, hb,
-    t3, s3, nu, nd, f1, f2, rsend, rrecv,
+    t3, s3, nu, nd, f1, f2, rsend, rrecv, sort, hp, ls, lr, lp, hs, hr, vbuf, khi, klo,
     sta, str_, stb,
     load_sem, wdx_sem, a_send, a_recv, g_send, g1, g3, gd,
-    h_sem, b_send, b_s, b_f, r_send, r_recv, st_send, st_recv, y_send, y1, y3, ym,
+    h_sem, b_send, b_s, b_f, r_send, r_recv, st_send, st_recv, y_send, y1, y3, ym, l_send, lm, lh,
 ):
     s = lax.axis_index("seq")
     cx = lax.axis_index("ctx")
@@ -175,14 +182,20 @@
             q = iota((ROWS, MSG * FLIGHT), 0)
             q = ((q * 205) >> 10) * (MSG - CAP) + q + CAP * rel
             unpack[rel] = jnp.where(q == iota((ROWS, MSG * FLIGHT), 1), 1.0, 0.0).astype(BF16)
+        q = iota((ROWS, 8 * ROWS), 0)
+        q = iota((ROWS, 8 * ROWS), 1) - ((q * 205) >> 10) * (PLACE - CAP) - q
+        for rel in range(4):
+            for c in range(2):
+                at = slice(SLOT[rel][c] * ROWS, (SLOT[rel][c] + 1) * ROWS)
+                sort[at, :] = jnp.where(q == (2 * rel + c) * CAP, 1.0, 0.0).astype(BF16)
         for cp in loads[1:4]:
             cp.wait()
-    with jax.named_scope("w_y1"):
-        for p in range(NP):
-            two = yb.at[p, pl.ds(0, 2)]
-            rcopy(two, two, y_send.at[0], y1.at[p], peer).wait_recv()
-            y_far(p, 1).start()
-            y_far(p, 3).start()
+
+    def y_relay(p):
+        two = yb.at[p, pl.ds(0, 2)]
+        rcopy(two, two, y_send.at[0], y1.at[p], peer).wait_recv()
+        y_far(p, 1).start()
+        y_far(p, 3).start()
 
     def y_message(p, i):
         ps, pe, pm = plane[i]
@@ -209,23 +222,26 @@
                 rcopy(most, most, y_send.at[1], ym.at[p], peer).wait_recv()
             got = yr[p].astype(F32).reshape(FLIGHT * MSG, C).astype(BF16)
             for rel in range(4):
-                xb[NR + p, 2 * rel + core] = dot(unpack[rel], got).astype(BF16)
+                xb[NR + p, slot(rel, core)] = dot(unpack[rel], got).astype(BF16)
                 g_peer(NR + p, rel).start()
 
+    def slot(rel, c):
+        return (c, 2 + 2 * c, 5 - 2 * c, 6 + c)[rel]
+
     def g_own_up(j):
-        return rcopy(xb.at[j, core], xb.at[j, 2 + core], g_send.at[0], g1.at[j], up)
+        return rcopy(xb.at[j, core], xb.at[j, slot(1, core)], g_send.at[0], g1.at[j], up)
 
     def g_own_down(j):
-        return rcopy(xb.at[j, core], xb.at[j, 4 + core], g_send.at[1], g1.at[j], down)
+        return rcopy(xb.at[j, core], xb.at[j, slot(2, core)], g_send.at[1], g1.at[j], down)
 
     def g_far_up(j):
-        return rcopy(xb.at[j, 2 + core, :, left], xb.at[j, 6 + core, :, left], g_send.at[2], g3.at[j], up)
+        return rcopy(xb.at[j, slot(1, core), :, left], xb.at[j, 6 + core, :, left], g_send.at[2], g3.at[j], up)
 
     def g_far_down(j):
-        return rcopy(xb.at[j, 4 + core, :, right], xb.at[j, 6 + core, :, right], g_send.at[3], g3.at[j], down)
+        return rcopy(xb.at[j, slot(2, core), :, right], xb.at[j, 6 + core, :, right], g_send.at[3], g3.at[j], down)
 
     def g_peer(j, rel):
-        at = 2 * rel + core
+        at = slot(rel, core)
         return rcopy(xb.at[j, at], xb.at[j, at], g_send.at[4 + rel], gd.at[rel // 3, j], peer)
 
     def g_peer_wait(j, rel):
@@ -247,163 +263,15 @@
         rcopy(xb.at[j, 0], xb.at[j, 0], g_send.at[0], g3.at[j], peer).wait_recv()
         g_peer(j, 3).start()
 
+    def multiply_near(j):
+        with jax.named_scope("w_d"):
+            g_peer_wait(j, 0)
+        for rel in range(3):
+            multiply(j, rel)
+
     def multiply_far(j):
         g_peer_wait(j, 3)
         multiply(j, 3)
-
-    def gather(i, carry):
-        @stage(i + AHEAD < NR, "disp")
-        def _():
-            dispatch(i + AHEAD)
-
-        @stage(i < NR, "fa")
-        def _():
-            j = i
-            with jax.named_scope("w_a"):
-                rcopy(
-                    asend.at[j, pl.ds(0, 15)], arecv.at[j, pl.ds(0, 15)], a_send, a_recv.at[j], peer
-                ).wait_recv()
-            got = arecv[j].astype(F32).reshape(TOKS, C).astype(BF16)
-            xb[j, core] = dot(sel[...], got).astype(BF16)
-            g_own_up(j).start()
-            g_own_down(j).start()
-            g_peer(j, 0).start()
-            cols = pl.ds(pl.multiple_of(j * C, 128), C)
-            logits[...] += dot(tok[:, cols], rw[cols, :])
-
-        @stage((i >= LAG) & (i < NR), "ff")
-        def _():
-            relay(i - LAG)
-
-        @stage((i >= NEAR) & (i < NR + NEAR), "fn")
-        def _():
-            j = i - NEAR
-            with jax.named_scope("w_g1"):
-                two = xb.at[j, pl.ds(0, 2)]
-                rcopy(two, two, g_send.at[0], g1.at[j], peer).wait_recv()
-            g_peer(j, 1).start()
-            g_peer(j, 2).start()
-
-        @stage(i == NR, "ff")
-        def _():
-            for j in range(NR - LAG, NR - NEAR + 1):
-                relay(j)
-
-        @stage(i == NR - AHEAD, "ymsg")
-        def _():
-            y_messages()
-
-        @stage(i == NR + 2, "yarr")
-        def _():
-            y_arrived()
-
-        @stage((i > NR) & (i < NR + NEAR), "ff")
-        def _():
-            relay(i - NEAR)
-
-        @stage((i >= NEAR + 2), "fm")
-        def _():
-            j = i - NEAR - 2
-            with jax.named_scope("w_d"):
-                g_peer_wait(j, 0)
-            for rel in range(3):
-                multiply(j, rel)
-
-        @stage((i >= LAG + 2) & (i < LAG + 2 + NR - LATE), "fc")
-        def _():
-            with jax.named_scope("w_g3"):
-                relay_arrived(i - LAG - 2)
-
-        @stage((i >= LAG + 4) & (i < LAG + 4 + NR - LATE), "fmf")
-        def _():
-            multiply_far(i - LAG - 4)
-
-        @stage(i >= NR + NEAR + 2, "fmf")
-        def _():
-            multiply_far(i - NEAR - 2)
-
-        return carry
-
-    lax.fori_loop(0, NC + NEAR + 2, gather, 0)
-
-    def hidden(lo, n, k):
-        at = pl.ds(lo, n)
-        gate = accg[at, :]
-        hb[core, at, :] = (gate * jax.nn.sigmoid(gate) * accu[at, :]).astype(BF16)
-        h_copy(lo, n, k, core).start()
-
-    def h_copy(lo, n, k, slot):
-        at = pl.ds(lo, n)
-        return rcopy(hb.at[core, at, :], hb.at[slot, at, :], h_sem.at[0, k], h_sem.at[1, k], peer)
-
-    near_rows, far_rows = 6 * ROWS, 2 * ROWS
-    with jax.named_scope("hn"):
-        hidden(0, near_rows, 0)
-    with jax.named_scope("w_h"):
-        loads[4].wait()
-        wdx.wait_recv()
-        h_copy(0, near_rows, 0, other).wait_recv()
-
-    def chunk(m):
-        return pl.ds(pl.multiple_of(m * CM, 128), CM)
-
-    def down_rows(lo, n, m):
-        at = slice(lo * ROWS, (lo + n) * ROWS)
-        cols = chunk(m)
-        return dot(hb[0, at, :], wd[0, :, cols]) + dot(hb[1, at, :], wd[1, :, cols])
-
-    def b_up(m, k):
-        return rcopy(nu.at[m, k], f1.at[m, k], b_send.at[k], b_f.at[m], up)
-
-    def b_down(m, k):
-        return rcopy(nd.at[m, k], f2.at[m, k], b_send.at[2 + k], b_f.at[m], down)
-
-    def b_far_up(m):
-        return rcopy(t3.at[0, m], s3.at[0, m], b_send.at[4], b_s.at[m], up)
-
-    def b_far_down(m):
-        return rcopy(t3.at[1, m], s3.at[1, m], b_send.at[5], b_s.at[m], down)
-
-    def independent(m):
-        nd[m, 0] = down_rows(2, 1, m).astype(BF16)
-        b_down(m, 0).start()
-        nu[m, 1] = down_rows(5, 1, m).astype(BF16)
-        b_up(m, 1).start()
-
-    def late(j):
-        with jax.named_scope("w_g3"):
-            relay_arrived(j)
-
-    def step(q, carry):
-        with jax.named_scope("ind"):
-            independent(q)
-
-        @stage(q >= 1, "late")
-        def _():
-            late(NR - LATE - 1 + q)
-
-        @stage(q >= 3, "fmf")
-        def _():
-            multiply_far(NR - LATE - 3 + q)
-
-        return carry
-
-    lax.fori_loop(0, LATE + 1, step, 0)
-    with jax.named_scope("fmf"):
-        multiply_far(NR - 2)
-        multiply_far(NR - 1)
-    with jax.named_scope("hf"):
-        hidden(near_rows, far_rows, 1)
-    with jax.named_scope("ind"):
-        for q in range(LATE + 1, FIRST):
-            independent(q)
-    with jax.named_scope("w_hf"):
-        h_copy(near_rows, far_rows, 1, other).wait_recv()
-
-    def r_copy(m, rel, i):
-        ps, pe, pm = plane[i]
-        cc = core if rel == 0 else other
-        return rcopy(rsend.at[m, cc, pm], rrecv.at[m, core * 16 + me], r_send.at[rel], r_recv.at[m], (ps, y * 2 + cc, pe))
 
     def st_a(i, rel):
         ps, pe, pm = plane[i]
@@ -433,7 +301,10 @@
         g = jnp.where(ghi[...].astype(F32) > 0.0, wide, 0.0)
         hi = g.astype(BF16)
         ghi[...] = hi
-        glo[...] = (g - hi.astype(F32)).astype(BF16)
+        lo = (g - hi.astype(F32)).astype(BF16)
+        glo[...] = lo
+        khi[...] = dot(hi, exd[...]).astype(BF16)
+        klo[...] = dot(lo, exd[...]).astype(BF16)
         for rel in range(2):
             for i in range(0, 16, 2):
                 if (rel, i) != (0, 0):
@@ -451,24 +322,249 @@
         for dev in (up, down, far):
             st_b(dev).start()
 
+    def gather(i, carry):
+        @stage(i + AHEAD < NR, "disp")
+        def _():
+            dispatch(i + AHEAD)
+
+        @stage(i < NR, "fa")
+        def _():
+            j = i
+            with jax.named_scope("w_a"):
+                rcopy(
+                    asend.at[j, pl.ds(0, 15)], arecv.at[j, pl.ds(0, 15)], a_send, a_recv.at[j], peer
+                ).wait_recv()
+            got = arecv[j].astype(F32).reshape(TOKS, C).astype(BF16)
+            xb[j, core] = dot(sel[...], got).astype(BF16)
+            g_own_up(j).start()
+            g_own_down(j).start()
+            g_peer(j, 0).start()
+            cols = pl.ds(pl.multiple_of(j * C, 128), C)
+            logits[...] += dot(tok[:, cols], rw[cols, :])
+
+        @stage(i < NP, "w_y1")
+        def _():
+            y_relay(i)
+
+        @stage((i >= LAG) & (i < NR), "ff")
+        def _():
+            relay(i - LAG)
+
+        @stage((i >= NEAR) & (i < NR + NEAR), "fn")
+        def _():
+            j = i - NEAR
+            with jax.named_scope("w_g1"):
+                two = xb.at[j, pl.ds(0, 2)]
+                rcopy(two, two, g_send.at[0], g1.at[j], peer).wait_recv()
+            g_peer(j, 1).start()
+            g_peer(j, 2).start()
+
+        @stage(i == NR, "ff")
+        def _():
+            for j in range(NR - LAG, NR - NEAR + 1):
+                relay(j)
+
+        @stage(i == NR - AHEAD, "ymsg")
+        def _():
+            y_messages()
+
+        @stage(i == NR, "yarr")
+        def _():
+            y_arrived()
+
+        @stage(i == NR + 1, "stat")
+        def _():
+            statistics()
+
+        @stage((i > NR) & (i < NR + NEAR), "ff")
+        def _():
+            relay(i - NEAR)
+
+        @stage((i > NEAR) & (i < NR + NEAR), "fm")
+        def _():
+            multiply_near(i - NEAR - 1)
+
+        @stage(i == NR + NEAR - 1, "fm")
+        def _():
+            for j in range(NR, NC):
+                multiply_near(j)
+
+        @stage(i == NR + NEAR, "fm")
+        def _():
+            multiply_near(NR - 1)
+
+        @stage(i >= FAR, "fc")
+        def _():
+            with jax.named_scope("w_g3"):
+                relay_arrived(i - FAR)
+
+        @stage((i > FAR) & (i <= FAR + EARLY), "fmf")
+        def _():
+            multiply_far(i - FAR - 1)
+
+        return carry
+
+    lax.fori_loop(0, NR + NEAR + 1, gather, 0)
+
+    def hidden(lo, n, k):
+        at = pl.ds(lo, n)
+        gate = accg[at, :]
+        hb[core, at, :] = (gate * jax.nn.sigmoid(gate) * accu[at, :]).astype(BF16)
+        h_copy(lo, n, k, core).start()
+
+    def h_copy(lo, n, k, slot):
+        at = pl.ds(lo, n)
+        return rcopy(hb.at[core, at, :], hb.at[slot, at, :], h_sem.at[0, k], h_sem.at[1, k], peer)
+
+    near_rows, far_rows = 6 * ROWS, 2 * ROWS
+    with jax.named_scope("hn"):
+        hidden(0, near_rows, 0)
+    with jax.named_scope("w_h"):
+        loads[4].wait()
+        wdx.wait_recv()
+        h_copy(0, near_rows, 0, other).wait_recv()
+
+    def chunk(m):
+        return pl.ds(pl.multiple_of(m * CM, 128), CM)
+
+    def down_rows(lo, n, m):
+        at = slice(lo * ROWS, (lo + n) * ROWS)
+        cols = chunk(m)
+        return dot(hb[0, at, :], wd[0, :, cols]) + dot(hb[1, at, :], wd[1, :, cols])
+
+    def rows_of(slots, m):
+        at = slice(slots * ROWS, (slots + 2) * ROWS)
+
+        @pl.when(m < NB)
+        def _():
+            vbuf[...] = down_rows(slots, 2, m)
+
+        @pl.when(m >= NB)
+        def _():
+            vbuf[...] = lp[m - NB, at, :].astype(F32)
+
+        return vbuf[...]
+
+    def l_copy(q, i):
+        ps, pe, pm = plane[i]
+        return rcopy(ls.at[q, pm], lr.at[q, me], l_send.at[0], lm.at[q], (ps, cx, pe))
+
+    def reorder():
+        q = iota((8 * ROWS, ROWS), 1)
+        q = iota((8 * ROWS, ROWS), 0) - ((q * 205) >> 10) * (PLACE - CAP) - q
+        for half in range(2):
+            v = jnp.zeros((8 * ROWS, HID), F32)
+            for rel in range(4):
+                for c in range(2):
+                    at = slice(SLOT[rel][c] * ROWS, (SLOT[rel][c] + 1) * ROWS)
+                    take = jnp.where(q == (2 * rel + c) * CAP, 1.0, 0.0).astype(BF16)
+                    v = v + dot(take, hb[half, at, :])
+            hp[half] = v.astype(BF16)
+
+    def go_home(q):
+        cols = chunk(NB + q)
+        v = dot(hp[0], wd[0, :, cols]) + dot(hp[1], wd[1, :, cols])
+        ls[q] = v.reshape(FLIGHT, PLACE, CM).astype(BF16)
+        for i in range(1, 16):
+            l_copy(q, i).start()
+        lr[q, me] = ls[q, me]
+
+    def came_home(q):
+        most = lr.at[q, pl.ds(0, 15)]
+        rcopy(most, most, l_send.at[0], lm.at[q], peer).wait_recv()
+        lp[q] = dot(sort[...], lr[q].reshape(8 * ROWS, CM)).astype(BF16)
+
+    def h_share(q):
+        return rcopy(hs.at[q], hr.at[q, core], l_send.at[1], lh.at[q], peer)
+
+    def b_up(m, k):
+        return rcopy(nu.at[m, k], f1.at[m, k], b_send.at[k], b_f.at[m], up)
+
+    def b_down(m, k):
+        return rcopy(nd.at[m, k], f2.at[m, k], b_send.at[2 + k], b_f.at[m], down)
+
+    def b_far_up(m):
+        return rcopy(t3.at[0, m], s3.at[0, m], b_send.at[4], b_s.at[m], up)
+
+    def b_far_down(m):
+        return rcopy(t3.at[1, m], s3.at[1, m], b_send.at[5], b_s.at[m], down)
+
+    def independent(m):
+        v = rows_of(2, m)
+        nd[m, 0] = v[:ROWS].astype(BF16)
+        b_down(m, 0).start()
+        nu[m, 1] = v[ROWS:].astype(BF16)
+        b_up(m, 1).start()
+
+    def ind(q):
+        with jax.named_scope("ind"):
+            independent(q)
+
+    waiting = [(j,) for j in range(NR + NEAR + 1 - FAR, NR)]
+    ready = list(range(EARLY, NR + NEAR + 1 - FAR)) + list(range(NR, NC))
+    ind(0)
+    for q in range(1, FIRST):
+        ind(q)
+        if waiting:
+            (j,) = waiting.pop(0)
+            with jax.named_scope("w_g3"):
+                relay_arrived(j)
+            ready.append(j)
+        with jax.named_scope("fmf"):
+            for j in ready[:2] if len(ready) > 2 else []:
+                multiply_far(j)
+            if len(ready) > 2:
+                ready = ready[2:]
+    with jax.named_scope("fmf"):
+        for (j,) in waiting:
+            relay_arrived(j)
+            ready.append(j)
+        for j in ready:
+            multiply_far(j)
+    with jax.named_scope("hf"):
+        hidden(near_rows, far_rows, 1)
+    with jax.named_scope("w_hf"):
+        h_copy(near_rows, far_rows, 1, other).wait_recv()
+
+    def r_copy(m, rel, i):
+        ps, pe, pm = plane[i]
+        cc = core if rel == 0 else other
+        return rcopy(rsend.at[m, cc, pm], rrecv.at[m, core * 16 + me], r_send.at[rel], r_recv.at[m], (ps, y * 2 + cc, pe))
+
     def backward(i, carry):
         @stage(i < NM, "bt")
         def _():
             m = i
-            v = down_rows(6, 2, m)
+            v = rows_of(6, m)
             t3[0, m] = v[:ROWS].astype(BF16)
             t3[1, m] = v[ROWS:].astype(BF16)
             b_far_up(m).start()
             b_far_down(m).start()
 
-        @stage((lax.rem(i, 2) == 1) & (i < 2 * (NM - FIRST)), "bi")
+        @stage((lax.rem(i, 2) == 1) & (i < 2 * (NB - FIRST)), "bi")
         def _():
             independent(FIRST + lax.div(i, 2))
 
+        @stage(i == 1, "home")
+        def _():
+            reorder()
+
+        @stage((i >= 1) & (i <= NL), "home")
+        def _():
+            go_home(i - 1)
+
+        @stage((i >= NB - NL) & (i < NB), "homew")
+        def _():
+            came_home(i - NB + NL)
+
+        @stage((i >= NB + LEAD) & (i < NM + LEAD), "bi")
+        def _():
+            independent(i - LEAD)
+
         @stage((i >= LEAD) & (i < NM + LEAD), "bb")
         def _():
             m = i - LEAD
-            v = down_rows(3, 2, m)
+            v = rows_of(4, m)
             with jax.named_scope("w_s"):
                 rcopy(nu.at[m], nu.at[m], b_send.at[0], b_s.at[m], peer).wait_recv()
             nu[m, 0] = (v[ROWS:] + s3[0, m].astype(F32)).astype(BF16)
@@ -476,33 +572,39 @@
             nd[m, 1] = (v[:ROWS] + s3[1, m].astype(F32)).astype(BF16)
             b_down(m, 1).start()
 
-        @stage(i == LEAD + 2, "stat")
-        def _():
-            statistics()
-
-        @stage(i == NM // 2, "stat")
+        @stage(i == LEAD - 1, "stat")
         def _():
             statistics_next()
 
         @stage((i >= LEAD + SUM) & (i < NM + LEAD + SUM), "bc")
         def _():
             m = i - LEAD - SUM
-            v = down_rows(0, 2, m)
+            v = rows_of(0, m)
             with jax.named_scope("w_f"):
                 four = nu.at[pl.ds(0, 2)]
                 rcopy(four, four, b_send.at[0], b_f.at[m], peer).wait_recv()
-            for cc in range(2):
-                at = slice(cc * ROWS, (cc + 1) * ROWS)
-                r = (v[at] + f1[m, cc].astype(F32) + f2[m, cc].astype(F32)).astype(BF16)
-                w = dot(exd[...], r)
-                rsend[m, cc] = w.reshape(FLIGHT, PAD, CM).astype(BF16)
-            for i2 in range(16):
-                for rel in range(2):
-                    if (rel, i2) != (0, 0):
-                        r_copy(m, rel, i2).start()
-            rrecv[m, core * 16 + me] = rsend[m, core, me]
-
-        @stage(i >= LEAD + BACK, "br")
+            r = [
+                (v[c * ROWS : (c + 1) * ROWS] + f1[m, c].astype(F32) + f2[m, c].astype(F32)).astype(BF16)
+                for c in range(2)
+            ]
+
+            @pl.when(m < NB)
+            def _():
+                for c in range(2):
+                    rsend[m, c] = dot(exd[...], r[c]).reshape(FLIGHT, PAD, CM).astype(BF16)
+                for i2 in range(16):
+                    for rel in range(2):
+                        if (rel, i2) != (0, 0):
+                            r_copy(m, rel, i2).start()
+                rrecv[m, core * 16 + me] = rsend[m, core, me]
+
+            @pl.when(m >= NB)
+            def _():
+                hs[m - NB] = jnp.where(core == 0, r[1], r[0])
+                h_share(m - NB).start()
+                hr[m - NB, core] = jnp.where(core == 0, r[0], r[1])
+
+        @stage((i >= LEAD + BACK) & (i < NB + LEAD + BACK), "br")
         def _():
             m = i - LEAD - BACK
             with jax.named_scope("w_r"):
@@ -515,7 +617,18 @@
 
         return carry
 
-    lax.fori_loop(0, NM + LEAD + BACK, backward, 0)
+    lax.fori_loop(0, max(NB + LEAD + BACK, NM + LEAD + SUM), backward, 0)
+
+    def last(q, carry):
+        with jax.named_scope("w_l"):
+            rcopy(hs.at[q], hr.at[q, other], l_send.at[1], lh.at[q], peer).wait_recv()
+        for half in range(2):
+            v = hr[q, half]
+            cols = pl.ds(pl.multiple_of(half * HALF + (NB + q) * CM, 128), CM)
+            out_ref[:, cols] = (dot(khi[...], v) + dot(klo[...], v)).astype(BF16)
+        return carry
+
+    lax.fori_loop(0, NL, last, 0)
 
     with jax.named_scope("fin"):
         all_b.wait_recv()
@@ -543,6 +656,8 @@
             left_(xb.at[:, core], g_send.at[4 + rel])
         for k in range(6):
             left_(t3.at[0], b_send.at[k])
+        left_(ls.at[:, pl.ds(0, 15)], l_send.at[0])
+        left_(hs, l_send.at[1])
         left_(rsend.at[:, 0, pl.ds(0, 15)], r_send.at[0])
         left_(rsend.at[:, 0], r_send.at[1])
 
@@ -589,8 +704,18 @@
             V((NM, 2, ROWS, CM), BF16),
             V((NM, 2, ROWS, CM), BF16),
             V((NM, 2, ROWS, CM), BF16),
-            V((NM, 2, FLIGHT, PAD, CM), BF16),
-            V((NM, 2 * FLIGHT, PAD, CM), BF16),
+            V((NB, 2, FLIGHT, PAD, CM), BF16),
+            V((NB, 2 * FLIGHT, PAD, CM), BF16),
+            V((8 * ROWS, 8 * ROWS), BF16),
+            V((2, 8 * ROWS, HID), BF16),
+            V((NL, FLIGHT, PLACE, CM), BF16),
+            V((NL, FLIGHT, PLACE, CM), BF16),
+            V((NL, 8 * ROWS, CM), BF16),
+            V((NL, ROWS, CM), BF16),
+            V((NL, 2, ROWS, CM), BF16),
+            V((2 * ROWS, CM), F32),
+            V((TOKS, ROWS), BF16),
+            V((TOKS, ROWS), BF16),
             V((2, 2, EXPERTS), F32),
             V((32, 2, EXPERTS), F32),
             V((4, 2, EXPERTS), F32),
@@ -607,13 +732,16 @@
             dma((NM,)),
             dma((NM,)),
             dma((2,)),
-            dma((NM,)),
+            dma((NB,)),
             dma((2,)),
             dma((2,)),
             dma((2,)),
             dma((NP,)),
             dma((NP,)),
             dma((NP,)),
+            dma((2,)),
+            dma((NL,)),
+            dma((NL,)),
         ],
         compiler_params=pltpu.CompilerParams(
             collective_id=0, has_side_effects=True, vmem_limit_bytes=52 * 1024 * 1024

time: 103 us -> 94 us (0.913)
  Pallas kernels: 100 us -> 90.7 us
    pallas_call x1, Pallas kernels: 100 us -> 90.7 us  [on_device(): pl.pallas_call(kernel, out_shape=(jax.ShapeDtypeStruct((TOKS, D), BF16),...]
where the time goes in v3:
time: 94 us; the launch traced here: 93.9 us
  Pallas kernels  90.7 us (96%)
  local copies, waits for them, and re-layouts  2.47 us (3%)
    pallas_call x1, Pallas kernels, on_device(): pl.pallas_call(kernel, out_shape=(jax.ShapeDtypeStruct((TOKS, D), BF16),...  90.7 us
    unnamed x4, local copies, waits for them, and re-layouts  2.47 us

profile of v3, /device:TPU:1, one launch (start us, length us, event | category | flops | bytes accessed | tf_op | source)
XLA Modules:
  0.0 93.9 jit_solution(15878339669404057491)
XLA Ops:
  0.6 0.0 copy-start
  0.6 0.7 copy-done
  1.3 90.7 %shard_map.77 = (bf16[128,7168]{1,0:T(8,128)(2,1)S(1)}, f32[1,256]{1,0:T(1,128)S(1)}) custom-call(bf16[128,7168]{1,0:T(8,128)(2,1)} %bitcast.13, s32[8,128]{1,0:T(8,128)S(1)} %bitcast.9, bf16[7168,256]{1,0:T(8,128)(2,1)} %rw_h.1, bf16[7168,256]{1,0:T(8,128)(2,1)} %bitcast.10, bf16[7168,256]{1,0:T(8,128)(2,1)} %bitcast.11, bf16[256,7168]{1,0:T(8,128)(2,1)} %bitcast.12), custom_call_target="tpu_custom_call" | custom-call | tf_op jit(solution)/shard_map/pallas_call | solution.py:670
  92.1 1.2 %copy.10 = bf16[1,128,7168]{2,1,0:T(8,128)(2,1)} copy(bf16[1,128,7168]{2,1,0:T(8,128)(2,1)S(1)} %bitcast.8) | data formatting | bytes 3670016
  93.3 0.6 copy.11
Async XLA Ops:
  0.6 0.7 copy-start

commit v4 on v3

--- a/solution.py
+++ b/solution.py
@@ -25,15 +25,16 @@
 NM, CM = 14, 256
 NR = 12
 NP = NC - NR
+YPRE = 2
+YARR = 0
 MSG = 24
 AHEAD = 6
 NEAR = 3
-LAG = 6
-FAR = 10
-EARLY = 3
+LAG = 8
+FAR = 12
+EARLY = 2
 NL = 3
 NB = NM - NL
-PLACE = 8 * CAP
 FIRST = 7
 LEAD = 3
 SUM = 3
@@ -66,10 +67,10 @@
     out_ref, bal_ref,
     tok, rw, wg, wu, wd, disp, sel, exd, pack, unpack, yb, ys, yr, ghi, glo, logits,
     asend, arecv, xb, accg, accu, hb,
-    t3, s3, nu, nd, f1, f2, rsend, rrecv, sort, hp, ls, lr, lp, hs, hr, vbuf, khi, klo,
+    t3, s3, nu, nd, f1, f2, rsend, rrecv, hp, ls, lr, lp, hr, vbuf, khi, klo,
     sta, str_, stb,
     load_sem, wdx_sem, a_send, a_recv, g_send, g1, g3, gd,
-    h_sem, b_send, b_s, b_f, r_send, r_recv, st_send, st_recv, y_send, y1, y3, ym, l_send, lm, lh,
+    h_sem, b_send, b_s, b_f, r_send, r_recv, st_send, st_recv, y_send, y1, y3, ym, l_send, lm,
 ):
     s = lax.axis_index("seq")
     cx = lax.axis_index("ctx")
@@ -123,14 +124,8 @@
     rank = dot(hit.astype(BF16), before)
     place = jnp.where(rank == (sub & 7).astype(F32), hit, 0.0)
     disp[...] = place.astype(BF16)
-    ghi[...] = place.T.astype(BF16)
     si, sl = iota((ROWS, TOKS), 0), iota((ROWS, TOKS), 1)
     sel[...] = jnp.where((si == (sl >> 3) * CAP + (sl & 7)) & ((sl & 7) < CAP), 1.0, 0.0).astype(BF16)
-    ei, el = iota((TOKS, ROWS), 1), iota((TOKS, ROWS), 0)
-    exd[...] = jnp.where((ei == (el >> 3) * CAP + (el & 7)) & ((el & 7) < CAP), 1.0, 0.0).astype(BF16)
-    logits[...] = jnp.zeros_like(logits)
-    accg[...] = jnp.zeros_like(accg)
-    accu[...] = jnp.zeros_like(accu)
 
     with jax.named_scope("w_bar"):
         pl.semaphore_wait(barrier, len(friends))
@@ -182,12 +177,12 @@
             q = iota((ROWS, MSG * FLIGHT), 0)
             q = ((q * 205) >> 10) * (MSG - CAP) + q + CAP * rel
             unpack[rel] = jnp.where(q == iota((ROWS, MSG * FLIGHT), 1), 1.0, 0.0).astype(BF16)
-        q = iota((ROWS, 8 * ROWS), 0)
-        q = iota((ROWS, 8 * ROWS), 1) - ((q * 205) >> 10) * (PLACE - CAP) - q
-        for rel in range(4):
-            for c in range(2):
-                at = slice(SLOT[rel][c] * ROWS, (SLOT[rel][c] + 1) * ROWS)
-                sort[at, :] = jnp.where(q == (2 * rel + c) * CAP, 1.0, 0.0).astype(BF16)
+        ei, el = iota((TOKS, ROWS), 1), iota((TOKS, ROWS), 0)
+        exd[...] = jnp.where((ei == (el >> 3) * CAP + (el & 7)) & ((el & 7) < CAP), 1.0, 0.0).astype(BF16)
+        logits[...] = jnp.zeros_like(logits)
+        accg[...] = jnp.zeros_like(accg)
+        accu[...] = jnp.zeros_like(accu)
+        ghi[...] = disp[...].astype(F32).T.astype(BF16)
         for cp in loads[1:4]:
             cp.wait()
 
@@ -197,33 +192,35 @@
         y_far(p, 1).start()
         y_far(p, 3).start()
 
+    with jax.named_scope("w_y1"):
+        for p in range(YPRE):
+            y_relay(p)
+
     def y_message(p, i):
         ps, pe, pm = plane[i]
         return rcopy(ys.at[p, pm], yr.at[p, me], y_send.at[1], ym.at[p], (ps, cx, pe))
 
-    def y_messages():
-        for p in range(NP):
-            with jax.named_scope("w_y3"):
-                rcopy(yb.at[p, 0], yb.at[p, 0], y_send.at[0], y3.at[p], peer).wait_recv()
-            v = dot(pack[0], yb[p, 0])
-            for rel in range(1, 4):
-                v = v + dot(pack[rel], yb[p, rel])
-            ys[p] = v.reshape(FLIGHT, MSG, C).astype(BF16)
-            for i in range(1, 16):
-                y_message(p, i).start()
-            yr[p, me] = ys[p, me]
-            cols = slice((NR + p) * C, (NR + p + 1) * C)
-            logits[...] += dot(tok[:, cols], rw[cols, :])
-
-    def y_arrived():
-        for p in range(NP):
-            with jax.named_scope("w_ym"):
-                most = yr.at[p, pl.ds(0, 15)]
-                rcopy(most, most, y_send.at[1], ym.at[p], peer).wait_recv()
-            got = yr[p].astype(F32).reshape(FLIGHT * MSG, C).astype(BF16)
-            for rel in range(4):
-                xb[NR + p, slot(rel, core)] = dot(unpack[rel], got).astype(BF16)
-                g_peer(NR + p, rel).start()
+    def y_messages(p):
+        with jax.named_scope("w_y3"):
+            rcopy(yb.at[p, 0], yb.at[p, 0], y_send.at[0], y3.at[p], peer).wait_recv()
+        v = dot(pack[0], yb[p, 0])
+        for rel in range(1, 4):
+            v = v + dot(pack[rel], yb[p, rel])
+        ys[p] = v.reshape(FLIGHT, MSG, C).astype(BF16)
+        for i in range(1, 16):
+            y_message(p, i).start()
+        yr[p, me] = ys[p, me]
+        cols = pl.ds(pl.multiple_of((NR + p) * C, 128), C)
+        logits[...] += dot(tok[:, cols], rw[cols, :])
+
+    def y_arrived(p):
+        with jax.named_scope("w_ym"):
+            most = yr.at[p, pl.ds(0, 15)]
+            rcopy(most, most, y_send.at[1], ym.at[p], peer).wait_recv()
+        got = yr[p].astype(F32).reshape(FLIGHT * MSG, C).astype(BF16)
+        for rel in range(4):
+            xb[NR + p, slot(rel, core)] = dot(unpack[rel], got).astype(BF16)
+            g_peer(NR + p, rel).start()
 
     def slot(rel, c):
         return (c, 2 + 2 * c, 5 - 2 * c, 6 + c)[rel]
@@ -342,9 +339,9 @@
             cols = pl.ds(pl.multiple_of(j * C, 128), C)
             logits[...] += dot(tok[:, cols], rw[cols, :])
 
-        @stage(i < NP, "w_y1")
-        def _():
-            y_relay(i)
+        @stage(i < NP - YPRE, "w_y1")
+        def _():
+            y_relay(i + YPRE)
 
         @stage((i >= LAG) & (i < NR), "ff")
         def _():
@@ -364,13 +361,13 @@
             for j in range(NR - LAG, NR - NEAR + 1):
                 relay(j)
 
-        @stage(i == NR - AHEAD, "ymsg")
-        def _():
-            y_messages()
-
-        @stage(i == NR, "yarr")
-        def _():
-            y_arrived()
+        @stage((i >= NR - AHEAD) & (i < NC - AHEAD), "ymsg")
+        def _():
+            y_messages(i - NR + AHEAD)
+
+        @stage((i >= NR - YARR) & (i < NC - YARR), "yarr")
+        def _():
+            y_arrived(i - NR + YARR)
 
         @stage(i == NR + 1, "stat")
         def _():
@@ -445,37 +442,38 @@
 
         return vbuf[...]
 
-    def l_copy(q, i):
+    def l_copy(q, rel, i):
         ps, pe, pm = plane[i]
-        return rcopy(ls.at[q, pm], lr.at[q, me], l_send.at[0], lm.at[q], (ps, cx, pe))
+        cc = core if rel == 0 else other
+        return rcopy(ls.at[q, cc, pm], lr.at[q, core * 16 + me], l_send, lm.at[q], (ps, y * 2 + cc, pe))
 
     def reorder():
-        q = iota((8 * ROWS, ROWS), 1)
-        q = iota((8 * ROWS, ROWS), 0) - ((q * 205) >> 10) * (PLACE - CAP) - q
         for half in range(2):
-            v = jnp.zeros((8 * ROWS, HID), F32)
-            for rel in range(4):
-                for c in range(2):
+            for c in range(2):
+                v = jnp.zeros((MSG * FLIGHT, HID), F32)
+                for rel in range(4):
                     at = slice(SLOT[rel][c] * ROWS, (SLOT[rel][c] + 1) * ROWS)
-                    take = jnp.where(q == (2 * rel + c) * CAP, 1.0, 0.0).astype(BF16)
-                    v = v + dot(take, hb[half, at, :])
-            hp[half] = v.astype(BF16)
+                    v = v + dot(pack[rel], hb[half, at, :])
+                hp[half, c * MSG * FLIGHT : (c + 1) * MSG * FLIGHT, :] = v.astype(BF16)
 
     def go_home(q):
         cols = chunk(NB + q)
         v = dot(hp[0], wd[0, :, cols]) + dot(hp[1], wd[1, :, cols])
-        ls[q] = v.reshape(FLIGHT, PLACE, CM).astype(BF16)
-        for i in range(1, 16):
-            l_copy(q, i).start()
-        lr[q, me] = ls[q, me]
+        ls[q] = v.reshape(2, FLIGHT, MSG, CM).astype(BF16)
+        for i in range(16):
+            for rel in range(2):
+                if (rel, i) != (0, 0):
+                    l_copy(q, rel, i).start()
+        lr[q, core * 16 + me] = ls[q, core, me]
 
     def came_home(q):
-        most = lr.at[q, pl.ds(0, 15)]
-        rcopy(most, most, l_send.at[0], lm.at[q], peer).wait_recv()
-        lp[q] = dot(sort[...], lr[q].reshape(8 * ROWS, CM)).astype(BF16)
-
-    def h_share(q):
-        return rcopy(hs.at[q], hr.at[q, core], l_send.at[1], lh.at[q], peer)
+        most = lr.at[q, pl.ds(0, 31)]
+        rcopy(most, most, l_send, lm.at[q], peer).wait_recv()
+        for half in range(2):
+            got = lr[q, half * 16 : half * 16 + 16].astype(F32).reshape(FLIGHT * MSG, CM).astype(BF16)
+            for rel in range(4):
+                at = slice(SLOT[rel][half] * ROWS, (SLOT[rel][half] + 1) * ROWS)
+                lp[q, at, :] = dot(unpack[rel], got).astype(BF16)
 
     def b_up(m, k):
         return rcopy(nu.at[m, k], f1.at[m, k], b_send.at[k], b_f.at[m], up)
@@ -500,23 +498,23 @@
         with jax.named_scope("ind"):
             independent(q)
 
-    waiting = [(j,) for j in range(NR + NEAR + 1 - FAR, NR)]
+    waiting = list(range(NR + NEAR + 1 - FAR, NR))
     ready = list(range(EARLY, NR + NEAR + 1 - FAR)) + list(range(NR, NC))
     ind(0)
     for q in range(1, FIRST):
         ind(q)
-        if waiting:
-            (j,) = waiting.pop(0)
+        for j in waiting[: 1 + (q > 2)]:
             with jax.named_scope("w_g3"):
                 relay_arrived(j)
             ready.append(j)
+        waiting = waiting[1 + (q > 2) :]
         with jax.named_scope("fmf"):
             for j in ready[:2] if len(ready) > 2 else []:
                 multiply_far(j)
             if len(ready) > 2:
                 ready = ready[2:]
     with jax.named_scope("fmf"):
-        for (j,) in waiting:
+        for j in waiting:
             relay_arrived(j)
             ready.append(j)
         for j in ready:
@@ -531,7 +529,17 @@
         cc = core if rel == 0 else other
         return rcopy(rsend.at[m, cc, pm], rrecv.at[m, core * 16 + me], r_send.at[rel], r_recv.at[m], (ps, y * 2 + cc, pe))
 
+    def last(q):
+        for half in range(2):
+            v = hr[q, half]
+            cols = pl.ds(pl.multiple_of(half * HALF + (NB + q) * CM, 128), CM)
+            out_ref[:, cols] = (dot(khi[...], v) + dot(klo[...], v)).astype(BF16)
+
     def backward(i, carry):
+        @stage((i >= NB) & (i < NM), "homew")
+        def _():
+            came_home(i - NB)
+
         @stage(i < NM, "bt")
         def _():
             m = i
@@ -552,10 +560,6 @@
         @stage((i >= 1) & (i <= NL), "home")
         def _():
             go_home(i - 1)
-
-        @stage((i >= NB - NL) & (i < NB), "homew")
-        def _():
-            came_home(i - NB + NL)
 
         @stage((i >= NB + LEAD) & (i < NM + LEAD), "bi")
         def _():
@@ -600,9 +604,12 @@
 
             @pl.when(m >= NB)
             def _():
-                hs[m - NB] = jnp.where(core == 0, r[1], r[0])
-                h_share(m - NB).start()
-                hr[m - NB, core] = jnp.where(core == 0, r[0], r[1])
+                for c in range(2):
+                    hr[m - NB, c] = r[c]
+
+        @stage((i >= NB + LEAD + SUM + 1) & (i < NM + LEAD + SUM), "last")
+        def _():
+            last(i - NB - LEAD - SUM - 1)
 
         @stage((i >= LEAD + BACK) & (i < NB + LEAD + BACK), "br")
         def _():
@@ -619,16 +626,7 @@
 
     lax.fori_loop(0, max(NB + LEAD + BACK, NM + LEAD + SUM), backward, 0)
 
-    def last(q, carry):
-        with jax.named_scope("w_l"):
-            rcopy(hs.at[q], hr.at[q, other], l_send.at[1], lh.at[q], peer).wait_recv()
-        for half in range(2):
-            v = hr[q, half]
-            cols = pl.ds(pl.multiple_of(half * HALF + (NB + q) * CM, 128), CM)
-            out_ref[:, cols] = (dot(khi[...], v) + dot(klo[...], v)).astype(BF16)
-        return carry
-
-    lax.fori_loop(0, NL, last, 0)
+    last(NL - 1)
 
     with jax.named_scope("fin"):
         all_b.wait_recv()
@@ -656,8 +654,7 @@
             left_(xb.at[:, core], g_send.at[4 + rel])
         for k in range(6):
             left_(t3.at[0], b_send.at[k])
-        left_(ls.at[:, pl.ds(0, 15)], l_send.at[0])
-        left_(hs, l_send.at[1])
+        left_(lr.at[:, pl.ds(0, 31)], l_send)
         left_(rsend.at[:, 0, pl.ds(0, 15)], r_send.at[0])
         left_(rsend.at[:, 0], r_send.at[1])
 
@@ -706,12 +703,10 @@
             V((NM, 2, ROWS, CM), BF16),
             V((NB, 2, FLIGHT, PAD, CM), BF16),
             V((NB, 2 * FLIGHT, PAD, CM), BF16),
-            V((8 * ROWS, 8 * ROWS), BF16),
-            V((2, 8 * ROWS, HID), BF16),
-            V((NL, FLIGHT, PLACE, CM), BF16),
-            V((NL, FLIGHT, PLACE, CM), BF16),
+            V((2, 2 * MSG * FLIGHT, HID), BF16),
+            V((NL, 2, FLIGHT, MSG, CM), BF16),
+            V((NL, 2 * FLIGHT, MSG, CM), BF16),
             V((NL, 8 * ROWS, CM), BF16),
-            V((NL, ROWS, CM), BF16),
             V((NL, 2, ROWS, CM), BF16),
             V((2 * ROWS, CM), F32),
             V((TOKS, ROWS), BF16),
@@ -739,8 +734,7 @@
             dma((NP,)),
             dma((NP,)),
             dma((NP,)),
-            dma((2,)),
-            dma((NL,)),
+            dma(()),
             dma((NL,)),
         ],
         compiler_params=pltpu.CompilerParams(

time: 94 us -> 92.7 us (0.986)
  Pallas kernels: 90.7 us -> 89.4 us
    pallas_call x1, Pallas kernels: 90.7 us -> 89.4 us  [on_device(): pl.pallas_call(kernel, out_shape=(jax.ShapeDtypeStruct((TOKS, D), BF16),...]
where the time goes in v4:
time: 92.7 us; the launch traced here: 92.5 us
  Pallas kernels  89.4 us (96%)
  local copies, waits for them, and re-layouts  2.47 us (3%)
    pallas_call x1, Pallas kernels, on_device(): pl.pallas_call(kernel, out_shape=(jax.ShapeDtypeStruct((TOKS, D), BF16),...  89.4 us
    unnamed x4, local copies, waits for them, and re-layouts  2.47 us

profile of v4, /device:TPU:1, one launch (start us, length us, event | category | flops | bytes accessed | tf_op | source)
XLA Modules:
  0.0 92.5 jit_solution(16397767651121174829)
XLA Ops:
  0.6 0.0 copy-start
  0.6 0.7 copy-done
  1.3 89.4 %shard_map.77 = (bf16[128,7168]{1,0:T(8,128)(2,1)S(1)}, f32[1,256]{1,0:T(1,128)S(1)}) custom-call(bf16[128,7168]{1,0:T(8,128)(2,1)} %bitcast.13, s32[8,128]{1,0:T(8,128)S(1)} %bitcast.9, bf16[7168,256]{1,0:T(8,128)(2,1)} %rw_h.1, bf16[7168,256]{1,0:T(8,128)(2,1)} %bitcast.10, bf16[7168,256]{1,0:T(8,128)(2,1)} %bitcast.11, bf16[256,7168]{1,0:T(8,128)(2,1)} %bitcast.12), custom_call_target="tpu_custom_call" | custom-call | tf_op jit(solution)/shard_map/pallas_call | solution.py:667
  90.7 1.2 %copy.10 = bf16[1,128,7168]{2,1,0:T(8,128)(2,1)} copy(bf16[1,128,7168]{2,1,0:T(8,128)(2,1)S(1)} %bitcast.8) | data formatting | bytes 3670016
  92.0 0.6 copy.11
Async XLA Ops:
  0.6 0.7 copy-start

commit v5 on v4

--- a/solution.py
+++ b/solution.py
@@ -38,7 +38,7 @@
 FIRST = 7
 LEAD = 3
 SUM = 3
-BACK = 9
+BACK = 8
 
 
 SLOT = ((0, 1), (2, 4), (5, 3), (6, 7))
@@ -109,9 +109,9 @@
         cp.start()
 
     barrier = pltpu.get_barrier_semaphore()
-    friends = [(ps, y * 2 + core, pe) for ps, pe, _ in plane[1:]]
-    friends += [(ps, y * 2 + other, pe) for ps, pe, _ in plane]
-    friends += [up, down, far]
+    away = sorted(range(16), key=lambda i: -(min(i // 4, 4 - i // 4) + 2 * (i // 2 % 2)))
+    friends = [(plane[i][0], y * 2 + c, plane[i][1]) for i in away for c in (other, core) if i or c is other]
+    friends += [far, up, down]
     for dev in friends:
         pl.semaphore_signal(barrier, inc=1, device_id=dev, device_id_type=MESH)
 
@@ -229,21 +229,21 @@
         return rcopy(xb.at[j, core], xb.at[j, slot(1, core)], g_send.at[0], g1.at[j], up)
 
     def g_own_down(j):
-        return rcopy(xb.at[j, core], xb.at[j, slot(2, core)], g_send.at[1], g1.at[j], down)
+        return rcopy(xb.at[j, core], xb.at[j, slot(2, core)], g_send.at[0], g1.at[j], down)
 
     def g_far_up(j):
-        return rcopy(xb.at[j, slot(1, core), :, left], xb.at[j, 6 + core, :, left], g_send.at[2], g3.at[j], up)
+        return rcopy(xb.at[j, slot(1, core), :, left], xb.at[j, 6 + core, :, left], g_send.at[0], g3.at[j], up)
 
     def g_far_down(j):
-        return rcopy(xb.at[j, slot(2, core), :, right], xb.at[j, 6 + core, :, right], g_send.at[3], g3.at[j], down)
+        return rcopy(xb.at[j, slot(2, core), :, right], xb.at[j, 6 + core, :, right], g_send.at[0], g3.at[j], down)
 
     def g_peer(j, rel):
         at = slot(rel, core)
-        return rcopy(xb.at[j, at], xb.at[j, at], g_send.at[4 + rel], gd.at[rel // 3, j], peer)
+        return rcopy(xb.at[j, at], xb.at[j, at], g_send.at[1], gd.at[rel // 3, j], peer)
 
     def g_peer_wait(j, rel):
         blocks = xb.at[j, pl.ds(0, 1 if rel == 3 else 3)]
-        rcopy(blocks, blocks, g_send.at[4], gd.at[rel // 3, j], peer).wait_recv()
+        rcopy(blocks, blocks, g_send.at[1], gd.at[rel // 3, j], peer).wait_recv()
 
     def multiply(j, rel):
         rows = pl.ds(pl.multiple_of(j * C, 128), C)
@@ -476,16 +476,16 @@
                 lp[q, at, :] = dot(unpack[rel], got).astype(BF16)
 
     def b_up(m, k):
-        return rcopy(nu.at[m, k], f1.at[m, k], b_send.at[k], b_f.at[m], up)
+        return rcopy(nu.at[m, k], f1.at[m, k], b_send, b_f.at[m], up)
 
     def b_down(m, k):
-        return rcopy(nd.at[m, k], f2.at[m, k], b_send.at[2 + k], b_f.at[m], down)
+        return rcopy(nd.at[m, k], f2.at[m, k], b_send, b_f.at[m], down)
 
     def b_far_up(m):
-        return rcopy(t3.at[0, m], s3.at[0, m], b_send.at[4], b_s.at[m], up)
+        return rcopy(t3.at[0, m], s3.at[0, m], b_send, b_s.at[m], up)
 
     def b_far_down(m):
-        return rcopy(t3.at[1, m], s3.at[1, m], b_send.at[5], b_s.at[m], down)
+        return rcopy(t3.at[1, m], s3.at[1, m], b_send, b_s.at[m], down)
 
     def independent(m):
         v = rows_of(2, m)
@@ -570,7 +570,7 @@
             m = i - LEAD
             v = rows_of(4, m)
             with jax.named_scope("w_s"):
-                rcopy(nu.at[m], nu.at[m], b_send.at[0], b_s.at[m], peer).wait_recv()
+                rcopy(nu.at[m], nu.at[m], b_send, b_s.at[m], peer).wait_recv()
             nu[m, 0] = (v[ROWS:] + s3[0, m].astype(F32)).astype(BF16)
             b_up(m, 0).start()
             nd[m, 1] = (v[:ROWS] + s3[1, m].astype(F32)).astype(BF16)
@@ -586,7 +586,7 @@
             v = rows_of(0, m)
             with jax.named_scope("w_f"):
                 four = nu.at[pl.ds(0, 2)]
-                rcopy(four, four, b_send.at[0], b_f.at[m], peer).wait_recv()
+                rcopy(four, four, b_send, b_f.at[m], peer).wait_recv()
             r = [
                 (v[c * ROWS : (c + 1) * ROWS] + f1[m, c].astype(F32) + f2[m, c].astype(F32)).astype(BF16)
                 for c in range(2)
@@ -643,20 +643,24 @@
             rcopy(src, src, sem, r_recv.at[0], peer).wait_send()
 
         left_(asend.at[:, pl.ds(0, 15)], a_send)
-        some = pl.ds(0, NR)
-        left_(xb.at[some, core], g_send.at[0])
-        left_(xb.at[some, core], g_send.at[1])
-        left_(xb.at[some, core, :, left], g_send.at[2])
-        left_(xb.at[some, core, :, left], g_send.at[3])
+        left_(xb.at[pl.ds(0, NR // 2), pl.ds(0, 6)], g_send.at[0])
+        left_(xb.at[:, pl.ds(0, 4)], g_send.at[1])
         left_(yb.at[:, pl.ds(0, 3)], y_send.at[0])
         left_(ys.at[:, pl.ds(0, 15)], y_send.at[1])
-        for rel in range(4):
-            left_(xb.at[:, core], g_send.at[4 + rel])
-        for k in range(6):
-            left_(t3.at[0], b_send.at[k])
+        left_(xb.at[pl.ds(0, NM // 2), pl.ds(0, 6)], b_send)
         left_(lr.at[:, pl.ds(0, 31)], l_send)
         left_(rsend.at[:, 0, pl.ds(0, 15)], r_send.at[0])
         left_(rsend.at[:, 0], r_send.at[1])
+
+
+def put_out(out_v, bal_v, out_h, bal_h, sem):
+    parts = [pl.ds(k * 16, 16) for k in range(TOKS // 16)]
+    copies = [pltpu.make_async_copy(out_v.at[p], out_h.at[p], sem.at[k]) for k, p in enumerate(parts)]
+    copies.append(pltpu.make_async_copy(bal_v, bal_h, sem.at[len(parts)]))
+    for cp in copies:
+        cp.start()
+    for cp in copies:
+        cp.wait()
 
 
 def on_device(tokens, routing, router_weight, w_gate, w_up, w_down):
@@ -718,12 +722,12 @@
             dma((2,)),
             dma(()),
             dma((NR,)),
-            dma((8,)),
+            dma((2,)),
             dma((NR,)),
             dma((NR,)),
             dma((2, NC)),
             dma((2, 2)),
-            dma((6,)),
+            dma(()),
             dma((NM,)),
             dma((NM,)),
             dma((2,)),
@@ -741,6 +745,17 @@
             collective_id=0, has_side_effects=True, vmem_limit_bytes=52 * 1024 * 1024
         ),
     )(tokens[0], routing[0].T, router_weight, w_gate[0], w_up[0], w_down[0])
+    out, bal = pl.pallas_call(
+        put_out,
+        out_shape=(
+            jax.ShapeDtypeStruct((TOKS, D), BF16),
+            jax.ShapeDtypeStruct((1, EXPERTS), F32),
+        ),
+        in_specs=[vmem, vmem],
+        out_specs=(hbm, hbm),
+        scratch_shapes=[dma((TOKS // 16 + 1,))],
+        compiler_params=pltpu.CompilerParams(vmem_limit_bytes=8 * 1024 * 1024),
+    )(out, bal)
     return out[None], bal
 
 

time: 92.7 us -> 91.9 us (level)
  local copies, waits for them, and re-layouts: 2.47 us -> 0.68 us
  Pallas kernels: 89.4 us -> 90.5 us
    unnamed x4 -> x2, local copies, waits for them, and re-layouts: 2.47 us -> 0.68 us
    pallas_call x0 -> x1, Pallas kernels: none -> 1.3 us  [on_device(): pl.pallas_call(put_out, out_shape=(jax.ShapeDtypeStruct((TOKS, D), BF16),...]
where the time goes in v5:
time: 91.9 us; the launch traced here: 91.8 us
  Pallas kernels  90.5 us (98%)
    pallas_call x1, Pallas kernels, on_device(): pl.pallas_call(kernel, out_shape=(jax.ShapeDtypeStruct((TOKS, D), BF16),...  89.2 us

profile of v5, /device:TPU:1, one launch (start us, length us, event | category | flops | bytes accessed | tf_op | source)
XLA Modules:
  0.0 91.8 jit_solution(4533235522961349660)
XLA Ops:
  0.6 0.0 copy-start
  0.6 0.7 copy-done
  1.3 89.2 %shard_map.77 = (bf16[128,7168]{1,0:T(8,128)(2,1)S(1)}, f32[1,256]{1,0:T(1,128)S(1)}) custom-call(bf16[128,7168]{1,0:T(8,128)(2,1)} %bitcast.12, s32[8,128]{1,0:T(8,128)S(1)} %bitcast.8, bf16[7168,256]{1,0:T(8,128)(2,1)} %rw_h.1, bf16[7168,256]{1,0:T(8,128)(2,1)} %bitcast.9, bf16[7168,256]{1,0:T(8,128)(2,1)} %bitcast.10, bf16[256,7168]{1,0:T(8,128)(2,1)} %bitcast.11), custom_call_target="tpu_custom_call" | custom-call | tf_op jit(solution)/shard_map/pallas_call | solution.py:671
  90.5 1.3 %shard_map.78 = (bf16[128,7168]{1,0:T(8,128)(2,1)}, f32[1,256]{1,0:T(1,128)}) custom-call(bf16[128,7168]{1,0:T(8,128)(2,1)S(1)} %get-tuple-element.6.out_v, f32[1,256]{1,0:T(1,128)S(1)} %get-tuple-element.7.bal_v), custom_call_target="tpu_custom_call" | custom-call | tf_op jit(solution)/shard_map/pallas_call | solution.py:748
Async XLA Ops:
  0.6 0.7 copy-start

commit v6 on v5

--- a/solution.py
+++ b/solution.py
@@ -65,7 +65,7 @@
 def kernel(
     tok_h, routes_ref, rw_h, wg_h, wu_h, wd_h,
     out_ref, bal_ref,
-    tok, rw, wg, wu, wd, disp, sel, exd, pack, unpack, yb, ys, yr, ghi, glo, logits,
+    tok, rw, wg, wu, wd, disp, sel, exd, pack, unpack, yb, ys, yr, ghi, both, logits,
     asend, arecv, xb, accg, accu, hb,
     t3, s3, nu, nd, f1, f2, rsend, rrecv, hp, ls, lr, lp, hr, vbuf, khi, klo,
     sta, str_, stb,
@@ -297,9 +297,9 @@
         wide = jnp.dot(weights, spread, preferred_element_type=F32, precision=lax.Precision.HIGHEST)
         g = jnp.where(ghi[...].astype(F32) > 0.0, wide, 0.0)
         hi = g.astype(BF16)
-        ghi[...] = hi
+        both[:, :TOKS] = hi
         lo = (g - hi.astype(F32)).astype(BF16)
-        glo[...] = lo
+        both[:, TOKS:] = lo
         khi[...] = dot(hi, exd[...]).astype(BF16)
         klo[...] = dot(lo, exd[...]).astype(BF16)
         for rel in range(2):
@@ -620,7 +620,7 @@
             for half in range(2):
                 v = rrecv[m, half * 16 : half * 16 + 16].astype(F32).reshape(TOKS, CM).astype(BF16)
                 cols = pl.ds(pl.multiple_of(half * HALF + m * CM, 128), CM)
-                out_ref[:, cols] = (dot(ghi[...], v) + dot(glo[...], v)).astype(BF16)
+                out_ref[:, cols] = dot(both[...], jnp.concatenate([v, v], axis=0)).astype(BF16)
 
         return carry
 
@@ -691,7 +691,7 @@
             V((NP, FLIGHT, MSG, C), BF16),
             V((NP, FLIGHT, MSG, C), BF16),
             V((TOKS, TOKS), BF16),
-            V((TOKS, TOKS), BF16),
+            V((TOKS, 2 * TOKS), BF16),
             V((TOKS, EXPERTS), F32),
             V((NR, FLIGHT, PAD, C), BF16),
             V((NR, FLIGHT, PAD, C), BF16),

time: 91.9 us -> 91.8 us (level)
  no operation moved by 1% of the time
where the time goes in v6:
time: 91.8 us; the launch traced here: 91.6 us
  Pallas kernels  90.3 us (98%)
    pallas_call x1, Pallas kernels, on_device(): pl.pallas_call(kernel, out_shape=(jax.ShapeDtypeStruct((TOKS, D), BF16),...  89 us

profile of v6, /device:TPU:1, one launch (start us, length us, event | category | flops | bytes accessed | tf_op | source)
XLA Modules:
  0.0 91.6 jit_solution(447508999618540283)
XLA Ops:
  0.6 0.0 copy-start
  0.6 0.7 copy-done
  1.3 89.0 %shard_map.77 = (bf16[128,7168]{1,0:T(8,128)(2,1)S(1)}, f32[1,256]{1,0:T(1,128)S(1)}) custom-call(bf16[128,7168]{1,0:T(8,128)(2,1)} %bitcast.12, s32[8,128]{1,0:T(8,128)S(1)} %bitcast.8, bf16[7168,256]{1,0:T(8,128)(2,1)} %rw_h.1, bf16[7168,256]{1,0:T(8,128)(2,1)} %bitcast.9, bf16[7168,256]{1,0:T(8,128)(2,1)} %bitcast.10, bf16[256,7168]{1,0:T(8,128)(2,1)} %bitcast.11), custom_call_target="tpu_custom_call" | custom-call | tf_op jit(solution)/shard_map/pallas_call | solution.py:671
  90.3 1.3 %shard_map.78 = (bf16[128,7168]{1,0:T(8,128)(2,1)}, f32[1,256]{1,0:T(1,128)}) custom-call(bf16[128,7168]{1,0:T(8,128)(2,1)S(1)} %get-tuple-element.6.out_v, f32[1,256]{1,0:T(1,128)S(1)} %get-tuple-element.7.bal_v), custom_call_target="tpu_custom_call" | custom-call | tf_op jit(solution)/shard_map/pallas_call | solution.py:748
Async XLA Ops:
  0.6 0.7 copy-start

commit v7 on v6

--- a/solution.py
+++ b/solution.py
@@ -139,8 +139,9 @@
         cols = pl.ds(pl.multiple_of(j * C, 128), C)
         rows = dot(disp[...], tok[:, cols])
         asend[j] = rows.reshape(FLIGHT, PAD, C).astype(BF16)
-        for i in range(1, 16):
-            a_copy(j, i).start()
+        for i in away:
+            if i:
+                a_copy(j, i).start()
         arecv[j, me] = asend[j, me]
 
     def dispatch_first(j, carry):
@@ -596,7 +597,7 @@
             def _():
                 for c in range(2):
                     rsend[m, c] = dot(exd[...], r[c]).reshape(FLIGHT, PAD, CM).astype(BF16)
-                for i2 in range(16):
+                for i2 in away:
                     for rel in range(2):
                         if (rel, i2) != (0, 0):
                             r_copy(m, rel, i2).start()

time: 91.8 us -> 95 us (1.035)
  Pallas kernels: 90.3 us -> 93.6 us
    pallas_call x1, Pallas kernels: 89 us -> 92.3 us  [on_device(): pl.pallas_call(kernel, out_shape=(jax.ShapeDtypeStruct((TOKS, D), BF16),...]
where the time goes in v7:
time: 95 us; the launch traced here: 94.9 us
  Pallas kernels  93.6 us (99%)
    pallas_call x1, Pallas kernels, on_device(): pl.pallas_call(kernel, out_shape=(jax.ShapeDtypeStruct((TOKS, D), BF16),...  92.3 us

profile of v7, /device:TPU:1, one launch (start us, length us, event | category | flops | bytes accessed | tf_op | source)
XLA Modules:
  0.0 94.9 jit_solution(10993806964108658402)
XLA Ops:
  0.6 0.0 copy-start
  0.6 0.7 copy-done
  1.3 92.3 %shard_map.77 = (bf16[128,7168]{1,0:T(8,128)(2,1)S(1)}, f32[1,256]{1,0:T(1,128)S(1)}) custom-call(bf16[128,7168]{1,0:T(8,128)(2,1)} %bitcast.12, s32[8,128]{1,0:T(8,128)S(1)} %bitcast.8, bf16[7168,256]{1,0:T(8,128)(2,1)} %rw_h.1, bf16[7168,256]{1,0:T(8,128)(2,1)} %bitcast.9, bf16[7168,256]{1,0:T(8,128)(2,1)} %bitcast.10, bf16[256,7168]{1,0:T(8,128)(2,1)} %bitcast.11), custom_call_target="tpu_custom_call" | custom-call | tf_op jit(solution)/shard_map/pallas_call | solution.py:672
  93.6 1.3 %shard_map.78 = (bf16[128,7168]{1,0:T(8,128)(2,1)}, f32[1,256]{1,0:T(1,128)}) custom-call(bf16[128,7168]{1,0:T(8,128)(2,1)S(1)} %get-tuple-element.6.out_v, f32[1,256]{1,0:T(1,128)S(1)} %get-tuple-element.7.bal_v), custom_call_target="tpu_custom_call" | custom-call | tf_op jit(solution)/shard_map/pallas_call | solution.py:749
Async XLA Ops:
  0.6 0.7 copy-start
